TPU v7x, 512 devices: a 8x2x16 block of a 8x16x16 slice. The times are simulated.
512 devices in a mesh: grp: 2 (over y), row: 16 (over z), col: 8 (over x), sub: 2 (over core).
Axes of the slice: x: 8, y: 2, z: 16, core: 2. Of those that a mesh axis runs over, the one named last changes fastest.
The devices are a block of a 8x16x16 slice.
Arguments:
- pair: bfloat16 [768, 384, 128], P(('grp', 'row'), ('col', 'sub')), parts along dimension 0, may hold values from -6 to 6
- chain_ids: int32 [768], P('grp'), parts along dimension 0, may hold values from 0 to 3, never falling along the last dimension, each value on 1 to 192 neighbouring positions
- residue_mask: int32 [768], P('grp'), parts along dimension 0, may hold values from 0 to 1, as said below
- chain_vec: float32 [128], replicated, may hold values from -4 to 4
- tri_in: bfloat16 [128, 512], replicated, may hold values from -0.5 to 0.5
- tri_gate: bfloat16 [128, 128], replicated, may hold values from -0.5 to 0.5
- tri_out: bfloat16 [128, 128], replicated, may hold values from -0.5 to 0.5
- att_query: bfloat16 [128, 256], replicated, may hold values from -0.5 to 0.5
- att_kv: bfloat16 [128, 256], replicated, may hold values from -0.5 to 0.5
- att_bias: bfloat16 [128, 4], replicated, may hold values from -0.5 to 0.5
- att_out: bfloat16 [128, 128], replicated, may hold values from -0.5 to 0.5
Outputs:
- updated: bfloat16 [768, 384, 128], P(('grp', 'row'), ('col', 'sub')), parts along dimension 0
There are 2 independent parts, one for each index of `grp`. A program takes and returns all parts, laid end to end along the dimension named above; an argument that names none is the same for every part. Nothing has to cross between parts.
Inputs may be any that keep to these rules, and one draw needn't show every extreme that they name: `chain_ids`: chains are runs of consecutive residues. `residue_mask`: 1 on residues 0 to L - 1 and 0 after them, with L between 192 and 384.
All inputs are finite; a program needn't handle non-finite values.
Results may differ from a plain program's by a relative error of at most 0.009.
Values may be sent and summed in bfloat16 or wider, within the bound.
No kernel may reach another device: no remote copies, remote signals or barrier semaphores. Data moves between devices by JAX's collectives and lax.ppermute only.
A program may use at most 64 MiB of HBM per device.

v0:
```python
import jax
import jax.numpy as jnp
from jax import lax
from jax.sharding import PartitionSpec as P

HEADS = 4
HEAD_DIM = 32


EPSILON = 1e-05


def laid_out(pieces, dim):
    pieces = jnp.moveaxis(pieces, 0, dim)
    dims = pieces.shape
    return pieces.reshape(*dims[:dim], dims[dim] * dims[dim + 1], *dims[dim + 2 :])


def from_everyone(array, axis):
    copies = jnp.broadcast_to(array, (lax.axis_size(axis), *array.shape))
    return lax.all_to_all(copies, axis, split_axis=0, concat_axis=0, tiled=True)


def collect(array, axis, dim):
    return laid_out(from_everyone(array, axis), dim)


def layer_norm(values):
    average = jnp.mean(values, axis=-1, keepdims=True)
    centred = values - average
    spread = jnp.mean(centred * centred, axis=-1, keepdims=True)
    return centred * lax.rsqrt(spread + EPSILON)


def on_device(
    pair,
    chain_ids,
    residue_mask,
    chain_vec,
    tri_in,
    tri_gate,
    tri_out,
    att_query,
    att_kv,
    att_bias,
    att_out,
):
    rows, cols, channels = pair.shape
    heads_width = HEADS * HEAD_DIM
    row_start = lax.axis_index("row") * rows
    col_block = lax.axis_index(("col", "sub"))
    col_start = col_block * cols
    living = residue_mask.astype(jnp.float32)
    row_live = lax.dynamic_slice_in_dim(living, row_start, rows)
    col_live = lax.dynamic_slice_in_dim(living, col_start, cols)
    row_chain = lax.dynamic_slice_in_dim(chain_ids, row_start, rows)
    col_chain = lax.dynamic_slice_in_dim(chain_ids, col_start, cols)
    same_chain = (row_chain[:, None] == col_chain[None, :]).astype(jnp.float32)
    pair_mask = row_live[:, None] * col_live[None, :]
    start_pair = pair.astype(jnp.float32) + same_chain[:, :, None] * chain_vec
    normed = layer_norm(start_pair).astype(jnp.bfloat16)
    flat_rows = normed.reshape(rows * cols, channels)
    projected = jnp.dot(flat_rows, tri_in, preferred_element_type=jnp.float32).reshape(
        rows, cols, 4 * channels
    )
    left_side = (
        jax.nn.sigmoid(projected[..., channels : 2 * channels])
        * projected[..., :channels]
        * pair_mask[..., None]
    )
    right_side = (
        jax.nn.sigmoid(projected[..., 3 * channels :])
        * projected[..., 2 * channels : 3 * channels]
        * pair_mask[..., None]
    )
    stacked = jnp.transpose(jnp.stack([left_side, right_side]).astype(jnp.bfloat16), (0, 3, 1, 2))
    regrouped = lax.all_to_all(
        lax.all_to_all(stacked, "row", split_axis=1, concat_axis=2, tiled=True),
        ("col", "sub"),
        split_axis=2,
        concat_axis=3,
        tiled=True,
    )
    left_part = regrouped[0]
    right_part = regrouped[1]
    product = jnp.einsum(
        "cjk,cik->cji",
        right_part,
        lax.all_gather(left_part, ("col", "sub"), axis=1, tiled=True),
        preferred_element_type=jnp.float32,
    ).astype(jnp.bfloat16)
    returned = lax.all_to_all(product, "row", split_axis=2, concat_axis=0, tiled=True)
    product_pairs = jnp.transpose(returned, (2, 1, 0)).astype(jnp.float32)
    tri_gating = jax.nn.sigmoid(
        jnp.dot(flat_rows, tri_gate, preferred_element_type=jnp.float32)
    ).reshape(rows, cols, channels)
    product_normed = layer_norm(product_pairs).astype(jnp.bfloat16)
    tri_update = tri_gating * jnp.dot(
        product_normed.reshape(-1, channels), tri_out, preferred_element_type=jnp.float32
    ).reshape(rows, cols, channels)
    after_tri = (start_pair + tri_update).astype(jnp.bfloat16)
    second = layer_norm(after_tri.astype(jnp.float32)).astype(jnp.bfloat16)
    flat_second = second.reshape(-1, channels)
    query_gate = jnp.dot(flat_second, att_query, preferred_element_type=jnp.float32).reshape(
        rows, cols, 2 * heads_width
    )
    query = (
        (query_gate[..., :heads_width] * HEAD_DIM ** (-0.5))
        .astype(jnp.bfloat16)
        .reshape(rows, cols, HEADS, HEAD_DIM)
    )
    gating = jax.nn.sigmoid(query_gate[..., heads_width:])
    local_bias = (
        jnp.dot(flat_second, att_bias, preferred_element_type=jnp.float32)
        .astype(jnp.bfloat16)
        .reshape(rows, cols, HEADS)
    )
    local_bias = jnp.transpose(local_bias, (2, 0, 1))
    groups = lax.axis_size(("col", "sub"))
    keyval_local = (
        jnp.dot(flat_second, att_kv, preferred_element_type=jnp.float32)
        .astype(jnp.bfloat16)
        .reshape(rows, cols, 2, HEADS, HEAD_DIM)
    )
    query_items = jnp.transpose(query, (2, 0, 1, 3)).reshape(HEADS * rows, cols, HEAD_DIM)
    key_items = jnp.transpose(keyval_local[:, :, 0], (2, 0, 1, 3)).reshape(
        HEADS * rows, cols, HEAD_DIM
    )
    value_items = jnp.transpose(keyval_local[:, :, 1], (2, 0, 1, 3)).reshape(
        HEADS * rows, cols, HEAD_DIM
    )
    item_stack = jnp.stack([query_items, key_items, value_items])
    whole_rows = lax.all_to_all(item_stack, ("col", "sub"), split_axis=1, concat_axis=2, tiled=True)
    repeated = jnp.repeat(local_bias, groups // HEADS, axis=0)
    bias_slab = lax.all_to_all(repeated, ("col", "sub"), split_axis=0, concat_axis=2, tiled=True)
    head_table = collect(bias_slab, "row", 1)
    head_bias = head_table[0].astype(jnp.float32)

    def attend_item(operands):
        query_one, key_one, value_one = operands
        scores = (
            jnp.einsum("jd,kd->jk", query_one, key_one, preferred_element_type=jnp.float32)
            + head_bias
        )
        weights = (jnp.exp(scores) * living[None, :]).astype(jnp.bfloat16)
        totals = jnp.sum(weights.astype(jnp.float32), axis=1)
        summed = jnp.dot(weights, value_one, preferred_element_type=jnp.float32)
        return summed / totals[:, None]

    item_results = lax.map(attend_item, (whole_rows[0], whole_rows[1], whole_rows[2]))
    back_items = lax.all_to_all(
        item_results.astype(jnp.bfloat16), ("col", "sub"), split_axis=1, concat_axis=0, tiled=True
    ).astype(item_results.dtype)
    attended = jnp.transpose(back_items.reshape(HEADS, rows, cols, HEAD_DIM), (1, 2, 0, 3))
    outgoing = (attended.reshape(rows, cols, heads_width) * gating).astype(jnp.bfloat16)
    result = after_tri.astype(jnp.float32) + jnp.dot(
        outgoing.reshape(-1, heads_width), att_out, preferred_element_type=jnp.float32
    ).reshape(rows, cols, channels)
    return result.astype(jnp.bfloat16)


def solution(mesh):
    return jax.shard_map(
        on_device,
        mesh=mesh,
        in_specs=(
            P(("grp", "row"), ("col", "sub"), None),
            P("grp"),
            P("grp"),
            P(),
            P(),
            P(),
            P(),
            P(),
            P(),
            P(),
            P(),
        ),
        out_specs=P(("grp", "row"), ("col", "sub"), None),
        check_vma=False,
    )
```

profile of v0, /device:TPU:65, one launch (start us, length us, event | category | flops | bytes accessed | tf_op | source)
XLA Modules:
  0.0 285.7 jit_solution(10988757312863492799)
XLA Ops:
  6.6 0.8 fusion.53
  7.5 1.2 fusion.36
  8.7 1.2 multiply_reduce_fusion.2
  9.9 1.2 multiply_convert_fusion.2
  12.5 0.9 copy.147
  13.4 2.1 reshape.183
  15.5 58.0 %all_to_all.89 = bf16[16,2,4608]{2,1,0:T(2,128)(2,1)S(1)} all-to-all(bf16[16,2,4608]{2,1,0:T(2,128)(2,1)S(1)} %reshape.183), channel_id=1, replica_groups=mesh['grp'=2,'row'=16,'col'=8,'sub'=2] {'row'}, dimensions={0} | all-to-all | bytes 589824 | tf_op jit(solution)/shard_map/all_to_all | solution.py:78
  73.6 2.2 reshape.184
  76.2 2.1 reshape.185
  78.3 25.6 %all_to_all.90 = bf16[16,2,4608]{2,1,0:T(2,128)(2,1)S(1)} all-to-all(bf16[16,2,4608]{2,1,0:T(2,128)(2,1)S(1)} %reshape.185), channel_id=1, replica_groups=mesh['grp'=2,'row'=16,'col'=8,'sub'=2] {'col','sub'}, dimensions={0} | all-to-all | bytes 589824 | tf_op jit(solution)/shard_map/all_to_all | solution.py:77
  103.9 2.2 reshape.186
  106.2 2.1 copy.181
  108.6 1.1 copy.153
  109.7 1.5 squeeze.32
  111.2 1.1 copy.152
  112.3 0.8 squeeze.31
  113.1 35.8 %all-gather.2.cloned.1.call-done = bf16[8,384,384]{2,1,0:T(8,128)(2,1)} async-done(((bf16[8,24,384]{2,1,0:T(8,128)(2,1)}), bf16[8,384,384]{2,1,0:T(8,128)(2,1)}) %all-gather.2.cloned.1.call-update) | async-done | bytes 2359312 | tf_op jit(solution)/shard_map/all_gather | solution.py:89
  148.8 2.6 convolution_convert_fusion.1
  151.9 1.7 reshape.187
  153.6 12.8 %all-to-all-start.2 = ((bf16[16,2,2304]{2,1,0:T(2,128)(2,1)}), bf16[16,2,2304]{2,1,0:T(2,128)(2,1)S(1)}, u32[]{:S(2)}, u32[]{:S(2)}) async-start(bf16[16,2,2304]{2,1,0:T(2,128)(2,1)} %reshape.187), calls=%async_computation.2 | async-start | bytes 294912 | tf_op jit(solution)/shard_map/all_to_all | solution.py:92
  166.7 11.7 %all-to-all-done.2 = bf16[16,2,2304]{2,1,0:T(2,128)(2,1)S(1)} async-done(((bf16[16,2,2304]{2,1,0:T(2,128)(2,1)}), bf16[16,2,2304]{2,1,0:T(2,128)(2,1)S(1)}, u32[]{:S(2)}, u32[]{:S(2)}) %all-to-all-start.2) | async-done | bytes 147488 | tf_op jit(solution)/shard_map/all_to_all | solution.py:92
  178.4 1.1 reshape.188
  183.6 0.8 copy.189
  184.8 0.8 copy.190
  186.0 1.1 fusion.44
  187.0 1.0 fusion.24
  188.3 0.8 copy.161
  189.8 0.8 reshape.191
  190.6 7.7 %all-to-all-start.4 = ((bf16[16,2,288]{2,1,0:T(2,128)(2,1)}), bf16[16,2,288]{2,1,0:T(2,128)(2,1)S(1)}, u32[]{:S(2)}, u32[]{:S(2)}) async-start(bf16[16,2,288]{2,1,0:T(2,128)(2,1)} %reshape.191), calls=%async_computation.4 | async-start | bytes 49152 | tf_op jit(solution)/shard_map/all_to_all | solution.py:135
  198.4 2.3 copy.164
  200.7 2.0 reshape.189
  202.7 3.0 %all-to-all-done.4 = bf16[16,2,288]{2,1,0:T(2,128)(2,1)S(1)} async-done(((bf16[16,2,288]{2,1,0:T(2,128)(2,1)}), bf16[16,2,288]{2,1,0:T(2,128)(2,1)S(1)}, u32[]{:S(2)}, u32[]{:S(2)}) %all-to-all-start.4) | async-done | bytes 18464 | tf_op jit(solution)/shard_map/all_to_all | solution.py:135
  205.7 4.3 %all-to-all-start.3 = ((bf16[16,2,6912]{2,1,0:T(2,128)(2,1)}), bf16[16,2,6912]{2,1,0:T(2,128)(2,1)S(1)}, u32[]{:S(2)}, u32[]{:S(2)}) async-start(bf16[16,2,6912]{2,1,0:T(2,128)(2,1)} %reshape.189), calls=%async_computation.3 | async-start | bytes 884736 | tf_op jit(solution)/shard_map/all_to_all | solution.py:133
  210.2 15.2 %all-to-all-done.3 = bf16[16,2,6912]{2,1,0:T(2,128)(2,1)S(1)} async-done(((bf16[16,2,6912]{2,1,0:T(2,128)(2,1)}), bf16[16,2,6912]{2,1,0:T(2,128)(2,1)S(1)}, u32[]{:S(2)}, u32[]{:S(2)}) %all-to-all-start.3) | async-done | bytes 442400 | tf_op jit(solution)/shard_map/all_to_all | solution.py:133
  226.2 4.9 %all-to-all-start.5 = ((bf16[16,1,24,384]{3,2,1,0:T(8,128)(2,1)}), bf16[16,1,24,384]{3,2,1,0:T(8,128)(2,1)S(1)}, u32[]{:S(2)}, u32[]{:S(2)}) async-start(bf16[16,1,24,384]{3,2,1,0:T(8,128)(2,1)} %broadcast_in_dim.11), calls=%async_computation.5 | async-start | bytes 589824 | tf_op jit(solution)/shard_map/all_to_all | solution.py:21
  231.1 1.0 reshape.190
  232.9 0.9 copy.184
  233.7 16.0 %all-to-all-done.5 = bf16[16,1,24,384]{3,2,1,0:T(8,128)(2,1)S(1)} async-done(((bf16[16,1,24,384]{3,2,1,0:T(8,128)(2,1)}), bf16[16,1,24,384]{3,2,1,0:T(8,128)(2,1)S(1)}, u32[]{:S(2)}, u32[]{:S(2)}) %all-to-all-start.5) | async-done | bytes 294944 | tf_op jit(solution)/shard_map/all_to_all | solution.py:21
  250.0 8.7 %while.10 = (s32[]{:T(128)}, bf16[6,384,32]{1,2,0:T(8,128)(2,1)S(1)}, bf16[6,384,32]{2,1,0:T(8,128)(2,1)S(1)}, bf16[6,384,32]{2,1,0:T(8,128)(2,1)S(1)}, f32[384,...) while((s32[]{:T(128)}, bf16[6,384,32]{1,2,0:T(8,128)(2,1)S(1)}, ...), condition=%wide.region_8.9_spmd, body=%wide.region_6.8_spmd.sunk | while | flops 19623552 | bytes 1531477 | solution.py:150
  250.4 1.1 fusion.72
  251.8 1.1 fusion.72
  253.3 1.1 fusion.72
  254.7 1.1 fusion.72
  256.2 1.1 fusion.72
  257.6 1.1 fusion.72
  259.9 13.2 %all_to_all.91 = bf16[16,2,2304]{2,1,0:T(2,128)(2,1)S(1)} all-to-all(bf16[16,2,2304]{2,1,0:T(2,128)(2,1)S(1)} %reshape.193), channel_id=1, replica_groups=mesh['grp'=2,'row'=16,'col'=8,'sub'=2] {'col','sub'}, dimensions={0} | all-to-all | bytes 294912 | tf_op jit(solution)/shard_map/all_to_all | solution.py:151
  274.0 0.9 reshape.178
  277.0 1.9 fusion.19
  (84 shorter events, 16.8 us)
Async XLA Ops:
  6.5 5.3 %copy-start = (bf16[128,512]{1,0:T(8,128)(2,1)S(1)}, bf16[128,512]{1,0:T(8,128)(2,1)}, u32[]{:S(2)}) copy-start(bf16[128,512]{1,0:T(8,128)(2,1)} %param.17) | copy-start | bytes 393220
  6.6 142.3 %all-gather.2.cloned.1.call-start = ((), (), s32[]{:S(2)}) async-start(), calls=%async_computation.7 | async-start | bytes 2506752 | tf_op jit(solution)/shard_map/all_gather | solution.py:89
  151.4 15.0 %copy-start.7 = (bf16[128,128]{1,0:T(8,128)(2,1)S(1)}, bf16[128,128]{1,0:T(8,128)(2,1)}, u32[]{:S(2)}) copy-start(bf16[128,128]{1,0:T(8,128)(2,1)} %param.18) | copy-start | bytes 98308
  153.6 24.8 %all-to-all-start.2 = ((bf16[16,2,2304]{2,1,0:T(2,128)(2,1)}), bf16[16,2,2304]{2,1,0:T(2,128)(2,1)S(1)}, u32[]{:S(2)}, u32[]{:S(2)}) async-start(bf16[16,2,2304]{2,1,0:T(2,128)(2,1)} %reshape.187), calls=%async_computation.2 | async-start | bytes 294912 | tf_op jit(solution)/shard_map/all_to_all | solution.py:92
  180.7 0.9 copy-start.1
  180.7 0.9 copy-start.4
  180.7 0.9 copy-start.5
  180.9 1.6 copy-start.3
  184.4 1.6 copy-start.2
  188.0 1.5 copy-start.6
  190.6 15.1 %all-to-all-start.4 = ((bf16[16,2,288]{2,1,0:T(2,128)(2,1)}), bf16[16,2,288]{2,1,0:T(2,128)(2,1)S(1)}, u32[]{:S(2)}, u32[]{:S(2)}) async-start(bf16[16,2,288]{2,1,0:T(2,128)(2,1)} %reshape.191), calls=%async_computation.4 | async-start | bytes 49152 | tf_op jit(solution)/shard_map/all_to_all | solution.py:135
  205.7 19.8 %all-to-all-start.3 = ((bf16[16,2,6912]{2,1,0:T(2,128)(2,1)}), bf16[16,2,6912]{2,1,0:T(2,128)(2,1)S(1)}, u32[]{:S(2)}, u32[]{:S(2)}) async-start(bf16[16,2,6912]{2,1,0:T(2,128)(2,1)} %reshape.189), calls=%async_computation.3 | async-start | bytes 884736 | tf_op jit(solution)/shard_map/all_to_all | solution.py:133
  226.2 23.5 %all-to-all-start.5 = ((bf16[16,1,24,384]{3,2,1,0:T(8,128)(2,1)}), bf16[16,1,24,384]{3,2,1,0:T(8,128)(2,1)S(1)}, u32[]{:S(2)}, u32[]{:S(2)}) async-start(bf16[16,1,24,384]{3,2,1,0:T(8,128)(2,1)} %broadcast_in_dim.11), calls=%async_computation.5 | async-start | bytes 589824 | tf_op jit(solution)/shard_map/all_to_all | solution.py:21
  275.7 1.3 copy-start.8
Sparse Core Ops, SparseCore 0:
  111.3 37.4 all-gather.1
where the time goes:
time: 287 us; the launch traced here: 286 us
  blocking collectives  96.8 us (34%)
  waiting for transfers between devices  81.7 us (28%)
  local copies, waits for them, and re-layouts  41.1 us (14%)
  starting transfers between devices  29.7 us (10%)
  matrix products  15.3 us (5%)
  between operations  14 us (5%)
  other arithmetic  7 us (2%)
    all_to_all x1, blocking collectives, on_device(): lax.all_to_all(stacked, 'row', split_axis=1, concat_axis=2, tiled=True)  58 us
    all_gather x1, waiting for transfers between devices, on_device(): lax.all_gather(left_part, ('col', 'sub'), axis=1, tiled=True)  35.8 us
    all_to_all x1, blocking collectives, on_device(): lax.all_to_all(lax.all_to_all(stacked, 'row', split_axis=1, concat_axis=2...  25.6 us
    unnamed x32, local copies, waits for them, and re-layouts  18.2 us
    all_to_all x1, waiting for transfers between devices, from_everyone(): return lax.all_to_all(copies, axis, split_axis=0, concat_axis=0, tiled=True)  16 us
    all_to_all x1, waiting for transfers between devices, on_device(): lax.all_to_all(item_stack, ('col', 'sub'), split_axis=1, concat_axis=2, t...  15.2 us
    all_to_all x1, blocking collectives, on_device(): lax.all_to_all(item_results.astype(jnp.bfloat16), ('col', 'sub'), split_a...  13.2 us
    all_to_all x1, starting transfers between devices, on_device(): lax.all_to_all(product, 'row', split_axis=2, concat_axis=0, tiled=True)  12.8 us
  transfers between devices with their start and end apart: 5, of which 5 were waited for; matrix products, arithmetic and copies ran while one was open for 3% of the time, Pallas kernels for 0%

commit v1 on v0

v1 whole, which is shorter than its diff:
```python
import jax
import jax.numpy as jnp
from jax import lax
from jax.experimental import pallas as pl
from jax.experimental.pallas import tpu as pltpu
from jax.sharding import PartitionSpec as P

HEADS = 4
HEAD_DIM = 32
EPSILON = 1e-05
LANES = 128
INTERPRET = False

F32 = jnp.float32
BF16 = jnp.bfloat16


def normalised(values):
    average = jnp.mean(values, axis=-1, keepdims=True)
    centred = values - average
    spread = jnp.mean(centred * centred, axis=-1, keepdims=True)
    return centred * lax.rsqrt(spread + EPSILON)


def sigmoid(values):
    return 1.0 / (1.0 + jnp.exp(-values))


def dot(a, b):
    return jnp.dot(a, b, preferred_element_type=F32)


def dot_t(a, b):
    return lax.dot_general(a, b, (((1,), (1,)), ((), ())), preferred_element_type=F32)


def lane_index(rows):
    return lax.broadcasted_iota(jnp.int32, (rows, LANES), 1)


def roll(values, shift):
    shift = shift % LANES
    return values if shift == 0 else pltpu.roll(values, shift, 1)


def call(kernel, outs, ins, spaces, scratch=(), flops=1 << 22):
    vmem = pl.BlockSpec(memory_space=pltpu.VMEM)
    smem = pl.BlockSpec(memory_space=pltpu.SMEM)
    return pl.pallas_call(
        kernel,
        out_shape=[jax.ShapeDtypeStruct(s, t) for s, t in outs],
        in_specs=[smem if k == "s" else vmem for k in spaces],
        out_specs=[vmem] * len(outs),
        scratch_shapes=list(scratch),
        interpret=INTERPRET,
        cost_estimate=pl.CostEstimate(flops=flops, transcendentals=0, bytes_accessed=1 << 20),
        name=kernel.__name__,
    )(*ins)


def start_block(pair_ref, chain_ref, live_ref, place_ref, vec_ref, rows, cols):
    row_start = place_ref[0]
    col_start = place_ref[1]
    spot = lax.broadcasted_iota(jnp.int32, (cols, LANES), 0)
    col_chain = jnp.zeros((cols, LANES), jnp.int32)
    col_live = jnp.zeros((cols, LANES), jnp.int32)
    for b in range(cols):
        col_chain = jnp.where(spot == b, chain_ref[col_start + b], col_chain)
        col_live = jnp.where(spot == b, live_ref[col_start + b], col_live)
    vec = jnp.broadcast_to(vec_ref[...], (cols, LANES))
    pieces, masks = [], []
    for a in range(rows):
        piece = pair_ref[a * cols : (a + 1) * cols, :].astype(F32)
        same = col_chain == chain_ref[row_start + a]
        pieces.append(piece + jnp.where(same, vec, 0.0))
        masks.append((col_live * live_ref[row_start + a]).astype(F32))
    return jnp.concatenate(pieces, axis=0), jnp.concatenate(masks, axis=0)


def sides_kernel(rows, cols, per_tile, tiles):
    def sides(pair_ref, chain_ref, live_ref, place_ref, vec_ref, tri_in_ref, send_ref):
        start, mask = start_block(pair_ref, chain_ref, live_ref, place_ref, vec_ref, rows, cols)
        normed = normalised(start).astype(BF16).astype(F32) * mask
        weights = tri_in_ref[...].astype(F32).T.astype(BF16)
        width = send_ref.shape[0]
        for t in range(tiles):
            low = t * per_tile * cols
            piece = normed[low : min(low + LANES, rows * cols)]
            if piece.shape[0] < LANES:
                piece = jnp.concatenate([piece, jnp.zeros((LANES - piece.shape[0], LANES), F32)], axis=0)
            projected = dot_t(weights, piece.astype(BF16))
            left = sigmoid(projected[width : 2 * width]) * projected[:width]
            right = sigmoid(projected[3 * width :]) * projected[2 * width : 3 * width]
            send_ref[:, t * LANES : (t + 1) * LANES] = left.astype(BF16)
            send_ref[:, (tiles + t) * LANES : (tiles + t + 1) * LANES] = right.astype(BF16)

    return sides


def gate_kernel(rows, cols):
    def gates(pair_ref, chain_ref, live_ref, place_ref, vec_ref, tri_gate_ref, query_ref, keyval_ref, start_ref, gate_ref, weights_ref):
        start, _ = start_block(pair_ref, chain_ref, live_ref, place_ref, vec_ref, rows, cols)
        start_ref[...] = start
        gate_ref[...] = sigmoid(dot(normalised(start).astype(BF16), tri_gate_ref[...]))
        width = HEADS * HEAD_DIM
        query = query_ref[:, :width].astype(F32)
        keys = keyval_ref[:, :width].astype(F32)
        values = keyval_ref[:, width:].astype(F32)
        lane = lane_index(query.shape[0])
        for h in range(HEADS):
            low = h * HEAD_DIM
            mixed = jnp.where(lane < HEAD_DIM, roll(query, -low), roll(keys, HEAD_DIM - low))
            mixed = jnp.where(lane < 2 * HEAD_DIM, mixed, roll(values, 2 * HEAD_DIM - low))
            mixed = jnp.where(lane < 3 * HEAD_DIM, mixed, 0.0)
            weights_ref[:, h * LANES : (h + 1) * LANES] = mixed.astype(BF16)

    return gates


def product_kernel(rows, cols, nrow, ncol, nsub, per_tile, tiles):
    blocks = nsub * ncol
    packed = LANES // 32
    groups = blocks // packed
    thirds = rows // 8
    length = nrow * rows

    def products(place_ref, gathered_ref, send_ref, left_ref, right_ref, pack_ref):
        sub = place_ref[2]
        lane = lane_index(nrow)

        def unpacked(side, g, a):
            low = (side * tiles + a // per_tile) * LANES
            offset = (a % per_tile) * cols
            mixed = jnp.zeros((nrow, LANES), F32)
            for q in range(packed):
                at = (g * packed + q) * nrow
                piece = gathered_ref[at : at + nrow, low : low + LANES].astype(F32)
                inside = (lane >= q * cols) & (lane < (q + 1) * cols)
                mixed = jnp.where(inside, roll(piece, q * cols - offset), mixed)
            return mixed

        for g in range(groups):
            for a in range(rows):
                left_ref[a * nrow : (a + 1) * nrow, g * LANES : (g + 1) * LANES] = unpacked(0, g, a).astype(BF16)
                right_ref[pl.ds(g * length + a, nrow, stride=rows), :] = unpacked(1, g, a)
        left = left_ref[...]
        for half in range(2):
            chosen = []
            for g in range(groups):
                parts = []
                for q in range(ncol // 2):
                    at = ((half * (ncol // 2) + q) * nsub + sub) * rows
                    parts.append(right_ref[pl.ds(pl.multiple_of(g * length + at, 8), rows), :])
                parts.append(jnp.zeros((LANES - rows * (ncol // 2), LANES), F32))
                chosen.append(jnp.concatenate(parts, axis=0))
            chosen = jnp.concatenate(chosen, axis=1).astype(BF16)
            found = dot_t(left, chosen)
            for q in range(ncol // 2):
                for u in range(8):
                    mixed = jnp.zeros((nrow, LANES), F32)
                    for v in range(thirds):
                        a = u * thirds + v
                        piece = found[a * nrow : (a + 1) * nrow]
                        inside = (lane >= v * cols) & (lane < (v + 1) * cols)
                        mixed = jnp.where(inside, roll(piece, v * cols - q * rows), mixed)
                    pack_ref[pl.ds(u, nrow, stride=8), :] = mixed
                at = (half * (ncol // 2) + q) * nrow * 8
                send_ref[at : at + nrow * 8, :] = pack_ref[...].astype(BF16)

    return products


def middle_kernel(rows, cols):
    def middle(back_ref, start_ref, gate_ref, tri_out_ref, weights_ref, query_ref, bias_ref, after_ref, gating_ref, items_ref, biases_ref, wide_ref):
        channels = back_ref.shape[0] // 8
        wide_ref[...] = back_ref[...].astype(F32)
        used = rows // 8 * cols
        parts = []
        for u in range(8):
            parts.append(wide_ref[pl.ds(u, channels, stride=8), :].T[:used])
        product = jnp.concatenate(parts, axis=0)
        product_normed = normalised(product).astype(BF16)
        after = (start_ref[...] + gate_ref[...] * dot(product_normed, tri_out_ref[...])).astype(BF16)
        after_ref[...] = after
        second = normalised(after.astype(F32)).astype(BF16)
        width = HEADS * HEAD_DIM
        biases_ref[...] = lax.dot_general(bias_ref[...], second, (((1,), (1,)), ((), ())), preferred_element_type=F32).astype(BF16)
        lane = lane_index(rows * cols)
        for h in range(HEADS):
            mixed = dot(second, weights_ref[:, h * LANES : (h + 1) * LANES])
            mixed = jnp.where(lane < HEAD_DIM, mixed * HEAD_DIM ** (-0.5), mixed)
            mixed = jnp.where(lane < 3 * HEAD_DIM, mixed, 1.0)
            items_ref[h * rows * cols : (h + 1) * rows * cols, :] = mixed.astype(BF16)
        gating_ref[...] = sigmoid(dot(second, query_ref[:, width:]))

    return middle


def attend_kernel(items, cols, blocks):
    length = blocks * cols

    def attend(whole_ref, bias_ref, live_ref, send_ref, slab_ref):
        bias = bias_ref[...].astype(F32)
        live = live_ref[...]
        lane = lane_index(length)
        slab_ref[...] = jnp.zeros(slab_ref.shape, F32)
        for a in range(items):
            piece = jnp.concatenate([whole_ref[m, a * cols : (a + 1) * cols, :].astype(F32) for m in range(blocks)], axis=0)
            query = piece[:, :HEAD_DIM].astype(BF16)
            keys = piece[:, HEAD_DIM : 2 * HEAD_DIM].astype(BF16)
            weights = (jnp.exp(dot_t(query, keys) + bias) * live).astype(BF16)
            summed = dot(weights, piece.astype(BF16))
            ratio = summed / roll(summed, -HEAD_DIM)
            group = a % 4
            inside = (lane >= group * HEAD_DIM) & (lane < (group + 1) * HEAD_DIM)
            slab_ref[a // 4] = jnp.where(inside, roll(ratio, (group - 2) * HEAD_DIM), slab_ref[a // 4])
        for part in range(slab_ref.shape[0]):
            for m in range(blocks):
                send_ref[m, part * cols : (part + 1) * cols, :] = slab_ref[part, m * cols : (m + 1) * cols, :].astype(BF16)

    return attend


def finish_kernel(rows, cols, items):
    def finish(back_ref, gating_ref, after_ref, att_out_ref, out_ref):
        lane = lane_index(cols)
        pieces = []
        for a in range(rows):
            group, item = a // items, a % items
            mixed = jnp.zeros((cols, LANES), F32)
            for h in range(HEADS):
                part = back_ref[h * (rows // items) + group, (item // 4) * cols : (item // 4 + 1) * cols, :].astype(F32)
                inside = (lane >= h * HEAD_DIM) & (lane < (h + 1) * HEAD_DIM)
                mixed = jnp.where(inside, roll(part, (h - item % 4) * HEAD_DIM), mixed)
            pieces.append(mixed)
        attended = jnp.concatenate(pieces, axis=0)
        outgoing = (attended * gating_ref[...]).astype(BF16)
        out_ref[...] = (after_ref[...].astype(F32) + dot(outgoing, att_out_ref[...])).astype(BF16)

    return finish


def on_device(
    pair, chain_ids, residue_mask, chain_vec, tri_in, tri_gate, tri_out, att_query, att_kv, att_bias, att_out
):
    rows, cols, channels = pair.shape
    nrow, ncol, nsub = lax.axis_size("row"), lax.axis_size("col"), lax.axis_size("sub")
    positions = rows * cols
    length = chain_ids.shape[0]
    blocks = ncol * nsub
    items = HEADS * rows // blocks
    per_tile = LANES // cols
    tiles = -(-rows // per_tile)
    place = jnp.stack([lax.axis_index("row") * rows, lax.axis_index(("col", "sub")) * cols, lax.axis_index("sub")]).astype(jnp.int32)
    flat = pair.reshape(positions, channels)
    vec = chain_vec.reshape(1, channels)
    common = (flat, chain_ids, residue_mask, place, vec)

    (send,) = call(sides_kernel(rows, cols, per_tile, tiles), [((channels, 2 * tiles * LANES), BF16)], common + (tri_in,), "vsssvv")
    moved = lax.all_to_all(send.reshape(channels, 2, tiles * LANES), ("col", "row"), split_axis=0, concat_axis=0, tiled=True)
    start, tri_gating, head_weights = call(
        gate_kernel(rows, cols),
        [((positions, channels), F32), ((positions, channels), F32), ((channels, HEADS * LANES), BF16)],
        common + (tri_gate, att_query, att_kv),
        "vsssvvvv",
    )
    gathered = lax.all_gather(moved.reshape(channels, 2 * tiles * LANES), "sub", axis=0, tiled=True)
    (products,) = call(
        product_kernel(rows, cols, nrow, ncol, nsub, per_tile, tiles),
        [((nrow * ncol * 8, LANES), BF16)],
        (place, gathered),
        "sv",
        scratch=[
            pltpu.VMEM((length, blocks // 4 * LANES), BF16),
            pltpu.VMEM((blocks // 4 * length, LANES), F32),
            pltpu.VMEM((nrow * 8, LANES), F32),
        ],
    )
    returned = lax.all_to_all(products.reshape(nrow * ncol, 8, LANES), ("col", "row"), split_axis=0, concat_axis=0, tiled=True)
    bias_rows = jnp.pad(att_bias.T, ((0, 8 - HEADS), (0, 0)))
    after, gating, sent_items, biases = call(
        middle_kernel(rows, cols),
        [((positions, channels), BF16), ((positions, channels), F32), ((HEADS * positions, LANES), BF16), ((8, positions), BF16)],
        (returned.reshape(channels * 8, LANES), start, tri_gating, tri_out, head_weights, att_query, bias_rows),
        "vvvvvvv",
        scratch=[pltpu.VMEM((channels * 8, LANES), F32)],
    )
    local_bias = biases[:HEADS].reshape(HEADS, rows, cols)
    repeated = jnp.repeat(local_bias, blocks // HEADS, axis=0)
    bias_slab = lax.all_to_all(repeated, ("col", "sub"), split_axis=0, concat_axis=2, tiled=True)
    copies = jnp.broadcast_to(bias_slab, (nrow, rows, length))
    head_table = lax.all_to_all(copies, "row", split_axis=0, concat_axis=0, tiled=True).reshape(length, length)
    whole = lax.all_to_all(
        sent_items.reshape(blocks, items * cols, LANES), ("col", "sub"), split_axis=0, concat_axis=0, tiled=True
    )
    slabs = -(-items // 4)
    (attended,) = call(
        attend_kernel(items, cols, blocks),
        [((blocks, slabs * cols, LANES), BF16)],
        (whole, head_table, residue_mask.astype(F32).reshape(1, length)),
        "vvv",
        scratch=[pltpu.VMEM((slabs, length, LANES), F32)],
    )
    back = lax.all_to_all(attended, ("col", "sub"), split_axis=0, concat_axis=0, tiled=True)
    (result,) = call(
        finish_kernel(rows, cols, items), [((positions, channels), BF16)], (back, gating, after, att_out), "vvvv"
    )
    return result.reshape(rows, cols, channels)


def solution(mesh):
    return jax.shard_map(
        on_device,
        mesh=mesh,
        in_specs=(P(("grp", "row"), ("col", "sub"), None), P("grp"), P("grp")) + (P(),) * 8,
        out_specs=P(("grp", "row"), ("col", "sub"), None),
        check_vma=False,
    )
```

time: 287 us -> 204 us (0.71)
  local copies, waits for them, and re-layouts: 41.1 us -> 6.36 us
  waiting for transfers between devices: 81.7 us -> 53 us
  Pallas kernels: 0 us -> 16.7 us
  matrix products: 15.3 us -> 0 us
  between operations: 14 us -> 0.1 us
  starting transfers between devices: 29.7 us -> 17.9 us
  blocking collectives: 96.8 us -> 108 us
  other arithmetic: 7 us -> 0.66 us
    all_gather x1 -> x0, waiting for transfers between devices: 35.8 us -> none  [on_device(): lax.all_gather(left_part, ('col', 'sub'), axis=1, tiled=True)]
    pallas_call x0 -> x6, Pallas kernels: none -> 16.7 us  [call(): pl.pallas_call(kernel, out_shape=[jax.ShapeDtypeStruct(s, t) for s, t in...]
    unnamed x32 -> x13, local copies, waits for them, and re-layouts: 18.2 us -> 2.41 us
    dot_general x20 -> x0, matrix products: 15.3 us -> none  [the longest x6 6.81 us: attend_item(): summed = jnp.dot(weights, value_one, preferred_element_type=jnp.float32)]
    all_to_all x4 -> x3, starting transfers between devices: 29.7 us -> 17.9 us  [the longest x1 9.91 us: on_device(): lax.all_to_all(products.reshape(nrow * ncol, 8, LANES), ('col', 'row'), s...]
    all_to_all x4 -> x3, waiting for transfers between devices: 45.9 us -> 53 us  [the longest x1 19.2 us: on_device(): lax.all_to_all(copies, 'row', split_axis=0, concat_axis=0, tiled=True)]
    all_to_all x3, blocking collectives: 96.8 us -> 103 us  [the longest x1 76.1 us: on_device(): lax.all_to_all(send.reshape(channels, 2, tiles * LANES), ('col', 'row'),...]
    all_gather x0 -> x1, blocking collectives: none -> 5.77 us  [on_device(): lax.all_gather(moved.reshape(channels, 2 * tiles * LANES), 'sub', axis=0,...]
  transfers between devices with their start and end apart: 5 -> 3, of which waited for: 5 -> 3; matrix products, arithmetic and copies ran while one was open for 3% -> 1% of each run, Pallas kernels for 0% -> 1%
where the time goes in v1:
time: 204 us; the launch traced here: 203 us
  blocking collectives  108 us (53%)
  waiting for transfers between devices  53 us (26%)
  starting transfers between devices  17.9 us (9%)
  Pallas kernels  16.7 us (8%)
  local copies, waits for them, and re-layouts  6.36 us (3%)
    all_to_all x1, blocking collectives, on_device(): lax.all_to_all(send.reshape(channels, 2, tiles * LANES), ('col', 'row'),...  76.1 us
    all_to_all x1, waiting for transfers between devices, on_device(): lax.all_to_all(copies, 'row', split_axis=0, concat_axis=0, tiled=True)  19.2 us
    all_to_all x1, waiting for transfers between devices, on_device(): lax.all_to_all(sent_items.reshape(blocks, items * cols, LANES), ('col', '...  17.9 us
    pallas_call x6, Pallas kernels, call(): pl.pallas_call(kernel, out_shape=[jax.ShapeDtypeStruct(s, t) for s, t in...  16.7 us
    all_to_all x1, waiting for transfers between devices, on_device(): lax.all_to_all(products.reshape(nrow * ncol, 8, LANES), ('col', 'row'), s...  15.8 us
    all_to_all x1, blocking collectives, on_device(): lax.all_to_all(attended, ('col', 'sub'), split_axis=0, concat_axis=0, til...  13.3 us
    all_to_all x1, blocking collectives, on_device(): lax.all_to_all(repeated, ('col', 'sub'), split_axis=0, concat_axis=2, til...  13.2 us
    all_to_all x1, starting transfers between devices, on_device(): lax.all_to_all(products.reshape(nrow * ncol, 8, LANES), ('col', 'row'), s...  9.91 us
  transfers between devices with their start and end apart: 3, of which 3 were waited for; matrix products, arithmetic and copies ran while one was open for 1% of the time, Pallas kernels for 1%

profile of v1, /device:TPU:65, one launch (start us, length us, event | category | flops | bytes accessed | tf_op | source)
XLA Modules:
  0.0 203.2 jit_solution(13402719845294639889)
XLA Ops:
  0.0 0.7 pad_add_fusion.place_ref
  0.7 2.4 %sides.1 = bf16[128,1280]{1,0:T(8,128)(2,1)} custom-call(bf16[576,128]{1,0:T(8,128)(2,1)} %bitcast.25, s32[384]{0:T(512)} %chain_ref.3, s32[384]{0:T(512)} %live_ref.3, s32[3]{0:T(128)} %pad_add_fusion.place_ref, f32[1,128]{1,0:T(1,128)} %bitcast.29, bf16[128,512]{1,0:T(8,128)(2,1)} %tri_in_ref.1), custom_call_target="tpu_custom_call" | custom-call | flops 4194304 | bytes 1048576 | tf_op jit(solution)/shard_map/sides/pallas_call | solution.py:49
  3.1 1.0 reshape.39
  4.1 76.1 %all_to_all.40 = bf16[128,2,640]{2,1,0:T(2,128)(2,1)S(1)} all-to-all(bf16[128,2,640]{2,1,0:T(2,128)(2,1)S(1)} %reshape.39), channel_id=1, replica_groups=mesh['grp'=2,'row'=16,'col'=8,'sub'=2] {'col','row'}, dimensions={0} | all-to-all | bytes 655360 | tf_op jit(solution)/shard_map/all_to_all | solution.py:260
  80.3 5.8 %all_gather.3.gathered_ref = bf16[256,1280]{1,0:T(8,128)(2,1)} all-gather(bf16[128,1280]{1,0:T(8,128)(2,1)S(1)} %bitcast.20), channel_id=1, replica_groups=mesh['grp'=2,'row'=16,'col'=8,'sub'=2] {'sub'}, dimensions={0}, use_global_device_ids=true | all-gather | bytes 983040 | tf_op jit(solution)/shard_map/all_gather | solution.py:267
  86.1 3.2 %products.1 = bf16[1024,128]{1,0:T(8,128)(2,1)} custom-call(s32[3]{0:T(128)} %pad_add_fusion.place_ref, bf16[256,1280]{1,0:T(8,128)(2,1)} %all_gather.3.gathered_ref), custom_call_target="tpu_custom_call" | custom-call | flops 4194304 | bytes 1048576 | tf_op jit(solution)/shard_map/products/pallas_call | solution.py:49
  89.3 9.9 %all-to-all-start.1 = ((bf16[128,8,128]{2,1,0:T(8,128)(2,1)}), bf16[128,8,128]{2,1,0:T(8,128)(2,1)S(1)}, u32[]{:S(2)}, u32[]{:S(2)}) async-start(bf16[128,8,128]{2,1,0:T(8,128)(2,1)} %bitcast.22), calls=%async_computation.1 | async-start | bytes 524288 | tf_op jit(solution)/shard_map/all_to_all | solution.py:279
  99.2 0.0 copy-start.4
  99.2 0.7 copy-done.4
  99.9 0.6 pad.4.bias_ref
  100.5 2.1 %gates.1 = (f32[576,128]{1,0:T(8,128)}, f32[576,128]{1,0:T(8,128)}, bf16[128,512]{1,0:T(8,128)(2,1)}) custom-call(bf16[576,128]{1,0:T(8,128)(2,1)} %bitcast.26, s32[384]{0:T(512)} %chain_ref.3, s32[384]{0:T(512)} %live_ref.3, s32[3]{0:T(128)} %pad_add_fusion.place_ref, f32[1,128]{1,0:T(1,128)} %bitcast.30, bf16[128,128]{1,0:T(8,128)(2,1)} %tri_gate_ref.1, ...), custom_call_target="tpu_custom_call" | custom-call | flops 4194304 | bytes 1048576 | tf_op jit(solution)/shard_map/gates/pallas_call | solution.py:49
  102.6 15.8 %all-to-all-done.1 = bf16[128,8,128]{2,1,0:T(8,128)(2,1)S(1)} async-done(((bf16[128,8,128]{2,1,0:T(8,128)(2,1)}), bf16[128,8,128]{2,1,0:T(8,128)(2,1)S(1)}, u32[]{:S(2)}, u32[]{:S(2)}) %all-to-all-start.1) | async-done | bytes 262176 | tf_op jit(solution)/shard_map/all_to_all | solution.py:279
  118.4 0.0 copy-start.2
  118.4 0.7 copy-done.2
  119.1 3.3 %middle.1 = (bf16[576,128]{1,0:T(8,128)(2,1)}, f32[576,128]{1,0:T(8,128)}, bf16[2304,128]{1,0:T(8,128)(2,1)}, bf16[8,576]{1,0:T(8,128)(2,1)}) custom-call(bf16[1024,128]{1,0:T(8,128)(2,1)} %bitcast.23, f32[576,128]{1,0:T(8,128)} %get-tuple-element.12.start_ref, f32[576,128]{1,0:T(8,128)} %get-tuple-element.13.gate_ref, bf16[128,128]{1,0:T(8,128)(2,1)} %tri_out_ref.1, ...), custom_call_target="tpu_custom_call" | custom-call | flops 4194304 | bytes 1048576 | tf_op jit(solution)/shard_map/middle/pallas_call | solution.py:49
  122.4 0.7 slice.3
  123.1 0.1 reshape.44
  123.2 0.2 reshape.49
  123.4 13.2 %all_to_all.41 = bf16[16,2,288]{2,1,0:T(2,128)(2,1)S(1)} all-to-all(bf16[16,2,288]{2,1,0:T(2,128)(2,1)S(1)} %reshape.49), channel_id=1, replica_groups=mesh['grp'=2,'row'=16,'col'=8,'sub'=2] {'col','sub'}, dimensions={0} | all-to-all | bytes 36864 | tf_op jit(solution)/shard_map/all_to_all | solution.py:290
  136.6 3.9 %all-to-all-start.2 = ((bf16[16,144,128]{2,1,0:T(8,128)(2,1)}), bf16[16,144,128]{2,1,0:T(8,128)(2,1)S(1)}, u32[]{:S(2)}, u32[]{:S(2)}) async-start(bf16[16,144,128]{2,1,0:T(8,128)(2,1)} %bitcast.24), calls=%async_computation.2 | async-start | bytes 1179648 | tf_op jit(solution)/shard_map/all_to_all | solution.py:293
  140.5 0.1 reshape.50
  140.7 0.1 broadcast_in_dim.11
  140.8 17.9 %all-to-all-done.2.whole_ref = bf16[16,144,128]{2,1,0:T(8,128)(2,1)S(1)} async-done(((bf16[16,144,128]{2,1,0:T(8,128)(2,1)}), bf16[16,144,128]{2,1,0:T(8,128)(2,1)S(1)}, u32[]{:S(2)}, u32[]{:S(2)}) %all-to-all-start.2) | async-done | bytes 589856 | tf_op jit(solution)/shard_map/all_to_all | solution.py:293
  158.8 0.0 copy-start
  158.8 0.8 broadcast_in_dim.12
  159.5 0.0 copy-start.3
  159.5 4.1 %all-to-all-start.4 = ((bf16[16,24,384]{2,1,0:T(8,128)(2,1)}), bf16[16,24,384]{2,1,0:T(8,128)(2,1)S(1)}, u32[]{:S(2)}, u32[]{:S(2)}) async-start(bf16[16,24,384]{2,1,0:T(8,128)(2,1)} %broadcast_in_dim.12), calls=%async_computation.4 | async-start | bytes 589824 | tf_op jit(solution)/shard_map/all_to_all | solution.py:292
  163.7 0.0 copy-done.3
  163.7 0.6 reshape.47.live_ref
  164.2 19.2 %all-to-all-done.4 = bf16[16,24,384]{2,1,0:T(8,128)(2,1)S(1)} async-done(((bf16[16,24,384]{2,1,0:T(8,128)(2,1)}), bf16[16,24,384]{2,1,0:T(8,128)(2,1)S(1)}, u32[]{:S(2)}, u32[]{:S(2)}) %all-to-all-start.4) | async-done | bytes 294944 | tf_op jit(solution)/shard_map/all_to_all | solution.py:292
  183.5 0.0 copy-start.1
  183.5 0.0 copy-done
  183.5 0.7 copy-done.1
  184.2 3.6 %attend.1 = bf16[16,48,128]{2,1,0:T(8,128)(2,1)} custom-call(bf16[16,144,128]{2,1,0:T(8,128)(2,1)} %copy-done, bf16[384,384]{1,0:T(8,128)(2,1)} %bitcast.21, f32[1,384]{1,0:T(1,128)} %reshape.47.live_ref), custom_call_target="tpu_custom_call" | custom-call | flops 4194304 | bytes 1048576 | tf_op jit(solution)/shard_map/attend/pallas_call | solution.py:49
  187.8 13.3 %all_to_all.42.back_ref = bf16[16,48,128]{2,1,0:T(8,128)(2,1)} all-to-all(bf16[16,48,128]{2,1,0:T(8,128)(2,1)} %attend.1), channel_id=1, replica_groups=mesh['grp'=2,'row'=16,'col'=8,'sub'=2] {'col','sub'}, dimensions={0} | all-to-all | bytes 393216 | tf_op jit(solution)/shard_map/all_to_all | solution.py:304
  201.1 2.1 %finish.1 = bf16[576,128]{1,0:T(8,128)(2,1)} custom-call(bf16[16,48,128]{2,1,0:T(8,128)(2,1)} %all_to_all.42.back_ref, f32[576,128]{1,0:T(8,128)} %get-tuple-element.17.gating_ref, bf16[576,128]{1,0:T(8,128)(2,1)} %get-tuple-element.18.after_ref, bf16[128,128]{1,0:T(8,128)(2,1)} %att_out_ref.1), custom_call_target="tpu_custom_call" | custom-call | flops 4194304 | bytes 1048576 | tf_op jit(solution)/shard_map/finish/pallas_call | solution.py:49
  (4 shorter events, 0.1 us)
Async XLA Ops:
  89.3 29.1 %all-to-all-start.1 = ((bf16[128,8,128]{2,1,0:T(8,128)(2,1)}), bf16[128,8,128]{2,1,0:T(8,128)(2,1)S(1)}, u32[]{:S(2)}, u32[]{:S(2)}) async-start(bf16[128,8,128]{2,1,0:T(8,128)(2,1)} %bitcast.22), calls=%async_computation.1 | async-start | bytes 524288 | tf_op jit(solution)/shard_map/all_to_all | solution.py:279
  99.2 0.7 copy-start.4
  118.4 0.7 copy-start.2
  136.6 22.2 %all-to-all-start.2 = ((bf16[16,144,128]{2,1,0:T(8,128)(2,1)}), bf16[16,144,128]{2,1,0:T(8,128)(2,1)S(1)}, u32[]{:S(2)}, u32[]{:S(2)}) async-start(bf16[16,144,128]{2,1,0:T(8,128)(2,1)} %bitcast.24), calls=%async_computation.2 | async-start | bytes 1179648 | tf_op jit(solution)/shard_map/all_to_all | solution.py:293
  158.8 24.7 %copy-start = (bf16[16,144,128]{2,1,0:T(8,128)(2,1)}, bf16[16,144,128]{2,1,0:T(8,128)(2,1)S(1)}, u32[]{:S(2)}) copy-start(bf16[16,144,128]{2,1,0:T(8,128)(2,1)S(1)} %all-to-all-done.2.whole_ref) | copy-start | bytes 1769476
  159.5 4.1 %copy-start.3 = (s32[384]{0:T(512)S(1)}, s32[384]{0:T(512)}, u32[]{:S(2)}) copy-start(s32[384]{0:T(512)} %live_ref.3) | copy-start | bytes 4612
  159.5 23.9 %all-to-all-start.4 = ((bf16[16,24,384]{2,1,0:T(8,128)(2,1)}), bf16[16,24,384]{2,1,0:T(8,128)(2,1)S(1)}, u32[]{:S(2)}, u32[]{:S(2)}) async-start(bf16[16,24,384]{2,1,0:T(8,128)(2,1)} %broadcast_in_dim.12), calls=%async_computation.4 | async-start | bytes 589824 | tf_op jit(solution)/shard_map/all_to_all | solution.py:292
  183.5 0.7 copy-start.1

commit v2 on v1

--- a/solution.py
+++ b/solution.py
@@ -53,6 +53,7 @@
         out_specs=[vmem] * len(outs),
         scratch_shapes=list(scratch),
         interpret=INTERPRET,
+        compiler_params=pltpu.CompilerParams(vmem_limit_bytes=16 << 20),
         cost_estimate=pl.CostEstimate(flops=flops, transcendentals=0, bytes_accessed=1 << 20),
         name=kernel.__name__,
     )(*ins)
@@ -121,10 +122,10 @@
     blocks = nsub * ncol
     packed = LANES // 32
     groups = blocks // packed
-    thirds = rows // 8
+    per_out = 4
     length = nrow * rows
 
-    def products(place_ref, gathered_ref, send_ref, left_ref, right_ref, pack_ref):
+    def products(place_ref, gathered_ref, send_ref, left_ref, right_ref):
         sub = place_ref[2]
         lane = lane_index(nrow)
 
@@ -156,44 +157,79 @@
             chosen = jnp.concatenate(chosen, axis=1).astype(BF16)
             found = dot_t(left, chosen)
             for q in range(ncol // 2):
-                for u in range(8):
+                at = (half * (ncol // 2) + q) * nrow
+                for u in range(rows // per_out):
                     mixed = jnp.zeros((nrow, LANES), F32)
-                    for v in range(thirds):
-                        a = u * thirds + v
+                    for v in range(per_out):
+                        a = u * per_out + v
                         piece = found[a * nrow : (a + 1) * nrow]
                         inside = (lane >= v * cols) & (lane < (v + 1) * cols)
                         mixed = jnp.where(inside, roll(piece, v * cols - q * rows), mixed)
-                    pack_ref[pl.ds(u, nrow, stride=8), :] = mixed
-                at = (half * (ncol // 2) + q) * nrow * 8
-                send_ref[at : at + nrow * 8, :] = pack_ref[...].astype(BF16)
+                    send_ref[at : at + nrow, u * LANES : (u + 1) * LANES] = mixed.astype(BF16)
 
     return products
 
 
-def middle_kernel(rows, cols):
-    def middle(back_ref, start_ref, gate_ref, tri_out_ref, weights_ref, query_ref, bias_ref, after_ref, gating_ref, items_ref, biases_ref, wide_ref):
-        channels = back_ref.shape[0] // 8
-        wide_ref[...] = back_ref[...].astype(F32)
-        used = rows // 8 * cols
+def middle_kernel(rows, cols, items, per_tile, tiles):
+    per_out = 4
+
+    def middle(back_ref, start_ref, gate_ref, tri_out_ref, weights_ref, query_ref, bias_ref, after_ref, gating_ref, items_ref, table_ref):
+        positions = rows * cols
         parts = []
-        for u in range(8):
-            parts.append(wide_ref[pl.ds(u, channels, stride=8), :].T[:used])
+        for u in range(rows // per_out):
+            parts.append(back_ref[:, u * LANES : (u + 1) * LANES].astype(F32).T[: per_out * cols])
         product = jnp.concatenate(parts, axis=0)
         product_normed = normalised(product).astype(BF16)
         after = (start_ref[...] + gate_ref[...] * dot(product_normed, tri_out_ref[...])).astype(BF16)
         after_ref[...] = after
-        second = normalised(after.astype(F32)).astype(BF16)
+        second_wide = normalised(after.astype(F32))
+        second = second_wide.astype(BF16)
         width = HEADS * HEAD_DIM
-        biases_ref[...] = lax.dot_general(bias_ref[...], second, (((1,), (1,)), ((), ())), preferred_element_type=F32).astype(BF16)
-        lane = lane_index(rows * cols)
+        spare = 3 * HEAD_DIM
+        lane = lane_index(8)
+        for t in range(tiles):
+            low = t * per_tile * cols
+            piece = second_wide[low : min(low + LANES, positions)]
+            if piece.shape[0] < LANES:
+                piece = jnp.concatenate([piece, jnp.zeros((LANES - piece.shape[0], LANES), F32)], axis=0)
+            found = dot_t(bias_ref[...], piece.astype(BF16))
+            for a in range(t * per_tile, min((t + 1) * per_tile, rows)):
+                moved = roll(found, spare - (a % per_tile) * cols)
+                table_ref[pl.ds(a, 8, stride=rows), :] = jnp.where((lane >= spare) & (lane < spare + cols), moved, 0.0)
+        lane = lane_index(positions)
         for h in range(HEADS):
             mixed = dot(second, weights_ref[:, h * LANES : (h + 1) * LANES])
             mixed = jnp.where(lane < HEAD_DIM, mixed * HEAD_DIM ** (-0.5), mixed)
-            mixed = jnp.where(lane < 3 * HEAD_DIM, mixed, 1.0)
-            items_ref[h * rows * cols : (h + 1) * rows * cols, :] = mixed.astype(BF16)
+            bias = table_ref[h * rows : (h + 1) * rows, :]
+            for group in range(rows // items):
+                low = group * items * cols
+                at = h * positions + low
+                items_ref[at : at + items * cols, :] = jnp.concatenate(
+                    [mixed[low : low + rows] + bias, mixed[low + rows : low + items * cols]], axis=0
+                ).astype(BF16)
         gating_ref[...] = sigmoid(dot(second, query_ref[:, width:]))
 
     return middle
+
+
+def table_kernel(rows, cols, blocks, copies):
+    def table(whole_ref, send_ref):
+        spare = 3 * HEAD_DIM
+        lane = lane_index(rows)
+        wide = blocks * cols // LANES
+        parts = [jnp.zeros((rows, LANES), F32) for _ in range(wide)]
+        for m in range(blocks):
+            piece = whole_ref[m, :rows, :].astype(F32)
+            moved = roll(piece, m * cols - spare)
+            for w in range(wide):
+                low, high = max(m * cols - w * LANES, 0), min((m + 1) * cols - w * LANES, LANES)
+                if low < high:
+                    parts[w] = jnp.where((lane >= low) & (lane < high), moved, parts[w])
+        whole = jnp.concatenate(parts, axis=1).astype(BF16)
+        for r in range(copies):
+            send_ref[r] = whole
+
+    return table
 
 
 def attend_kernel(items, cols, blocks):
@@ -209,7 +245,7 @@
             query = piece[:, :HEAD_DIM].astype(BF16)
             keys = piece[:, HEAD_DIM : 2 * HEAD_DIM].astype(BF16)
             weights = (jnp.exp(dot_t(query, keys) + bias) * live).astype(BF16)
-            summed = dot(weights, piece.astype(BF16))
+            summed = dot(weights, jnp.where(lane < 3 * HEAD_DIM, piece, 1.0).astype(BF16))
             ratio = summed / roll(summed, -HEAD_DIM)
             group = a % 4
             inside = (lane >= group * HEAD_DIM) & (lane < (group + 1) * HEAD_DIM)
@@ -267,32 +303,28 @@
     gathered = lax.all_gather(moved.reshape(channels, 2 * tiles * LANES), "sub", axis=0, tiled=True)
     (products,) = call(
         product_kernel(rows, cols, nrow, ncol, nsub, per_tile, tiles),
-        [((nrow * ncol * 8, LANES), BF16)],
+        [((nrow * ncol, rows // 4 * LANES), BF16)],
         (place, gathered),
         "sv",
         scratch=[
             pltpu.VMEM((length, blocks // 4 * LANES), BF16),
             pltpu.VMEM((blocks // 4 * length, LANES), F32),
-            pltpu.VMEM((nrow * 8, LANES), F32),
         ],
     )
-    returned = lax.all_to_all(products.reshape(nrow * ncol, 8, LANES), ("col", "row"), split_axis=0, concat_axis=0, tiled=True)
+    returned = lax.all_to_all(products.reshape(nrow * ncol, 2, rows // 8 * LANES), ("col", "row"), split_axis=0, concat_axis=0, tiled=True)
     bias_rows = jnp.pad(att_bias.T, ((0, 8 - HEADS), (0, 0)))
-    after, gating, sent_items, biases = call(
-        middle_kernel(rows, cols),
-        [((positions, channels), BF16), ((positions, channels), F32), ((HEADS * positions, LANES), BF16), ((8, positions), BF16)],
-        (returned.reshape(channels * 8, LANES), start, tri_gating, tri_out, head_weights, att_query, bias_rows),
+    after, gating, sent_items = call(
+        middle_kernel(rows, cols, items, per_tile, tiles),
+        [((positions, channels), BF16), ((positions, channels), F32), ((HEADS * positions, LANES), BF16)],
+        (returned.reshape(channels, rows // 4 * LANES), start, tri_gating, tri_out, head_weights, att_query, bias_rows),
         "vvvvvvv",
-        scratch=[pltpu.VMEM((channels * 8, LANES), F32)],
-    )
-    local_bias = biases[:HEADS].reshape(HEADS, rows, cols)
-    repeated = jnp.repeat(local_bias, blocks // HEADS, axis=0)
-    bias_slab = lax.all_to_all(repeated, ("col", "sub"), split_axis=0, concat_axis=2, tiled=True)
-    copies = jnp.broadcast_to(bias_slab, (nrow, rows, length))
-    head_table = lax.all_to_all(copies, "row", split_axis=0, concat_axis=0, tiled=True).reshape(length, length)
+        scratch=[pltpu.VMEM((8 * rows, LANES), F32)],
+    )
     whole = lax.all_to_all(
         sent_items.reshape(blocks, items * cols, LANES), ("col", "sub"), split_axis=0, concat_axis=0, tiled=True
     )
+    (copies,) = call(table_kernel(rows, cols, blocks, nrow), [((nrow, rows, length), BF16)], (whole,), "v")
+    head_table = lax.all_to_all(copies, "row", split_axis=0, concat_axis=0, tiled=True).reshape(length, length)
     slabs = -(-items // 4)
     (attended,) = call(
         attend_kernel(items, cols, blocks),

time: 204 us -> 183 us (0.90)
  waiting for transfers between devices: 53 us -> 31 us
  blocking collectives: 108 us -> 123 us
  Pallas kernels: 16.7 us -> 8.79 us
  starting transfers between devices: 17.9 us -> 14 us
    all_to_all x2 -> x1, waiting for transfers between devices: 33.7 us -> 15.1 us  [on_device(): lax.all_to_all(products.reshape(nrow * ncol, 2, rows // 8 * LANES), ('col...]
    all_to_all x1, blocking collectives: 13.2 us -> 24.5 us  [on_device(): lax.all_to_all(sent_items.reshape(blocks, items * cols, LANES), ('col', '...]
    pallas_call x6 -> x7, Pallas kernels: 16.7 us -> 8.79 us  [call(): pl.pallas_call(kernel, out_shape=[jax.ShapeDtypeStruct(s, t) for s, t in...]
    all_to_all x2 -> x1, starting transfers between devices: 13.8 us -> 10.1 us  [on_device(): lax.all_to_all(products.reshape(nrow * ncol, 2, rows // 8 * LANES), ('col...]
    all_to_all x1, blocking collectives: 13.3 us -> 16.9 us  [on_device(): lax.all_to_all(attended, ('col', 'sub'), split_axis=0, concat_axis=0, til...]
    all_to_all x1, waiting for transfers between devices: 19.2 us -> 15.9 us  [on_device(): lax.all_to_all(copies, 'row', split_axis=0, concat_axis=0, tiled=True)]
  transfers between devices with their start and end apart: 3 -> 2, of which waited for: 3 -> 2; matrix products, arithmetic and copies ran while one was open for 1% -> 0% of each run, Pallas kernels for 1% -> 1%
where the time goes in v2:
time: 183 us; the launch traced here: 182 us
  blocking collectives  123 us (67%)
  waiting for transfers between devices  31 us (17%)
  starting transfers between devices  14 us (8%)
  Pallas kernels  8.79 us (5%)
  local copies, waits for them, and re-layouts  4.79 us (3%)
    all_to_all x1, blocking collectives, on_device(): lax.all_to_all(send.reshape(channels, 2, tiles * LANES), ('col', 'row'),...  76.1 us
    all_to_all x1, blocking collectives, on_device(): lax.all_to_all(sent_items.reshape(blocks, items * cols, LANES), ('col', '...  24.5 us
    all_to_all x1, blocking collectives, on_device(): lax.all_to_all(attended, ('col', 'sub'), split_axis=0, concat_axis=0, til...  16.9 us
    all_to_all x1, waiting for transfers between devices, on_device(): lax.all_to_all(copies, 'row', split_axis=0, concat_axis=0, tiled=True)  15.9 us
    all_to_all x1, waiting for transfers between devices, on_device(): lax.all_to_all(products.reshape(nrow * ncol, 2, rows // 8 * LANES), ('col...  15.1 us
    all_to_all x1, starting transfers between devices, on_device(): lax.all_to_all(products.reshape(nrow * ncol, 2, rows // 8 * LANES), ('col...  10.1 us
    pallas_call x7, Pallas kernels, call(): pl.pallas_call(kernel, out_shape=[jax.ShapeDtypeStruct(s, t) for s, t in...  8.79 us
    all_gather x1, blocking collectives, on_device(): lax.all_gather(moved.reshape(channels, 2 * tiles * LANES), 'sub', axis=0,...  5.64 us
  transfers between devices with their start and end apart: 2, of which 2 were waited for; matrix products, arithmetic and copies ran while one was open for 0% of the time, Pallas kernels for 1%

profile of v2, /device:TPU:65, one launch (start us, length us, event | category | flops | bytes accessed | tf_op | source)
XLA Modules:
  0.0 181.9 jit_solution(15293225862692506917)
XLA Ops:
  0.0 0.0 copy-start.9
  0.0 0.1 pad_add_fusion.place_ref
  0.1 0.0 copy-start.8
  0.1 0.0 copy-start.10
  0.1 0.6 copy-done.9
  0.7 0.1 copy-done.8
  0.8 0.0 copy-done.10
  0.8 0.0 copy-start
  0.8 0.9 copy-done
  1.7 0.0 copy-start.3
  1.7 0.9 copy-done.3
  2.6 1.3 sides.1
  3.9 0.1 reshape.32
  4.0 76.1 %all_to_all.25 = bf16[128,2,640]{2,1,0:T(2,128)(2,1)S(1)} all-to-all(bf16[128,2,640]{2,1,0:T(2,128)(2,1)S(1)} %reshape.32), channel_id=1, replica_groups=mesh['grp'=2,'row'=16,'col'=8,'sub'=2] {'col','row'}, dimensions={0} | all-to-all | bytes 655360 | tf_op jit(solution)/shard_map/all_to_all | solution.py:296
  80.1 5.6 %all_gather.3.gathered_ref = bf16[256,1280]{1,0:T(8,128)(2,1)S(1)} all-gather(bf16[128,1280]{1,0:T(8,128)(2,1)S(1)} %bitcast.21), channel_id=1, replica_groups=mesh['grp'=2,'row'=16,'col'=8,'sub'=2] {'sub'}, dimensions={0}, use_global_device_ids=true | all-gather | bytes 983040 | tf_op jit(solution)/shard_map/all_gather | solution.py:303
  85.8 1.8 products.1
  87.6 0.7 reshape.34
  88.3 0.0 copy-start.1
  88.3 0.0 copy-start.2
  88.3 0.0 copy-start.4
  88.3 0.0 copy-start.5
  88.3 10.1 %all-to-all-start.1 = ((bf16[128,2,384]{2,1,0:T(2,128)(2,1)}), bf16[128,2,384]{2,1,0:T(2,128)(2,1)S(1)}, u32[]{:S(2)}, u32[]{:S(2)}) async-start(bf16[128,2,384]{2,1,0:T(2,128)(2,1)} %reshape.34), calls=%async_computation.1 | async-start | bytes 393216 | tf_op jit(solution)/shard_map/all_to_all | solution.py:314
  98.4 0.0 copy-start.11
  98.4 0.7 copy-done.11
  99.1 0.0 copy-done.1
  99.1 0.0 copy-done.2
  99.1 0.0 copy-done.4
  99.1 0.0 copy-done.5
  99.1 1.0 gates.1
  100.1 15.1 %all-to-all-done.1 = bf16[128,2,384]{2,1,0:T(2,128)(2,1)S(1)} async-done(((bf16[128,2,384]{2,1,0:T(2,128)(2,1)}), bf16[128,2,384]{2,1,0:T(2,128)(2,1)S(1)}, u32[]{:S(2)}, u32[]{:S(2)}) %all-to-all-start.1) | async-done | bytes 196640 | tf_op jit(solution)/shard_map/all_to_all | solution.py:314
  115.2 0.0 copy-start.6
  115.2 0.7 copy-done.6
  116.0 1.1 middle.1
  117.1 24.5 %all_to_all.26.whole_ref = bf16[16,144,128]{2,1,0:T(8,128)(2,1)S(1)} all-to-all(bf16[16,144,128]{2,1,0:T(8,128)(2,1)S(1)} %bitcast.15), channel_id=1, replica_groups=mesh['grp'=2,'row'=16,'col'=8,'sub'=2] {'col','sub'}, dimensions={0} | all-to-all | bytes 1179648 | tf_op jit(solution)/shard_map/all_to_all | solution.py:323
  141.6 0.8 table.1
  142.4 4.0 %all-to-all-start.3 = ((bf16[16,24,384]{2,1,0:T(8,128)(2,1)}), bf16[16,24,384]{2,1,0:T(8,128)(2,1)S(1)}, u32[]{:S(2)}, u32[]{:S(2)}) async-start(bf16[16,24,384]{2,1,0:T(8,128)(2,1)} %table.1), calls=%async_computation.3 | async-start | bytes 589824 | tf_op jit(solution)/shard_map/all_to_all | solution.py:327
  146.4 15.9 %all-to-all-done.3 = bf16[16,24,384]{2,1,0:T(8,128)(2,1)S(1)} async-done(((bf16[16,24,384]{2,1,0:T(8,128)(2,1)}), bf16[16,24,384]{2,1,0:T(8,128)(2,1)S(1)}, u32[]{:S(2)}, u32[]{:S(2)}) %all-to-all-start.3) | async-done | bytes 294944 | tf_op jit(solution)/shard_map/all_to_all | solution.py:327
  162.3 1.8 attend.1
  164.1 0.0 copy-start.7
  164.1 16.9 %all_to_all.27.back_ref = bf16[16,48,128]{2,1,0:T(8,128)(2,1)S(1)} all-to-all(bf16[16,48,128]{2,1,0:T(8,128)(2,1)S(1)} %attend.1), channel_id=1, replica_groups=mesh['grp'=2,'row'=16,'col'=8,'sub'=2] {'col','sub'}, dimensions={0} | all-to-all | bytes 393216 | tf_op jit(solution)/shard_map/all_to_all | solution.py:336
  181.0 0.0 copy-done.7
  181.0 1.0 finish.1
  (5 shorter events, 0.1 us)
Async XLA Ops:
  0.0 0.7 copy-start.9
  0.1 0.7 copy-start.8
  0.1 0.7 copy-start.10
  0.8 0.9 copy-start
  1.7 0.9 copy-start.3
  88.3 10.8 %copy-start.1 = (bf16[24,24,128]{2,1,0:T(8,128)(2,1)S(1)}, bf16[24,24,128]{2,1,0:T(8,128)(2,1)}, u32[]{:S(2)}) copy-start(bf16[24,24,128]{2,1,0:T(8,128)(2,1)} %param.11) | copy-start | bytes 442372
  88.3 10.8 %copy-start.2 = (bf16[128,256]{1,0:T(8,128)(2,1)S(1)}, bf16[128,256]{1,0:T(8,128)(2,1)}, u32[]{:S(2)}) copy-start(bf16[128,256]{1,0:T(8,128)(2,1)} %query_ref.3) | copy-start | bytes 196612
  88.3 10.8 %copy-start.4 = (bf16[128,256]{1,0:T(8,128)(2,1)S(1)}, bf16[128,256]{1,0:T(8,128)(2,1)}, u32[]{:S(2)}) copy-start(bf16[128,256]{1,0:T(8,128)(2,1)} %keyval_ref.1) | copy-start | bytes 196612
  88.3 10.8 %copy-start.5 = (bf16[128,128]{1,0:T(8,128)(2,1)S(1)}, bf16[128,128]{1,0:T(8,128)(2,1)}, u32[]{:S(2)}) copy-start(bf16[128,128]{1,0:T(8,128)(2,1)} %tri_gate_ref.1) | copy-start | bytes 98308
  88.3 26.9 %all-to-all-start.1 = ((bf16[128,2,384]{2,1,0:T(2,128)(2,1)}), bf16[128,2,384]{2,1,0:T(2,128)(2,1)S(1)}, u32[]{:S(2)}, u32[]{:S(2)}) async-start(bf16[128,2,384]{2,1,0:T(2,128)(2,1)} %reshape.34), calls=%async_computation.1 | async-start | bytes 393216 | tf_op jit(solution)/shard_map/all_to_all | solution.py:314
  98.4 0.7 copy-start.11
  115.2 0.8 copy-start.6
  142.4 19.9 %all-to-all-start.3 = ((bf16[16,24,384]{2,1,0:T(8,128)(2,1)}), bf16[16,24,384]{2,1,0:T(8,128)(2,1)S(1)}, u32[]{:S(2)}, u32[]{:S(2)}) async-start(bf16[16,24,384]{2,1,0:T(8,128)(2,1)} %table.1), calls=%async_computation.3 | async-start | bytes 589824 | tf_op jit(solution)/shard_map/all_to_all | solution.py:327
  164.1 16.9 %copy-start.7 = (bf16[128,128]{1,0:T(8,128)(2,1)S(1)}, bf16[128,128]{1,0:T(8,128)(2,1)}, u32[]{:S(2)}) copy-start(bf16[128,128]{1,0:T(8,128)(2,1)} %att_out_ref.1) | copy-start | bytes 98308

commit v3 on v2

--- a/solution.py
+++ b/solution.py
@@ -170,10 +170,10 @@
     return products
 
 
-def middle_kernel(rows, cols, items, per_tile, tiles):
+def after_kernel(rows, cols, copies, per_tile, tiles):
     per_out = 4
 
-    def middle(back_ref, start_ref, gate_ref, tri_out_ref, weights_ref, query_ref, bias_ref, after_ref, gating_ref, items_ref, table_ref):
+    def after(back_ref, start_ref, gate_ref, tri_out_ref, bias_ref, after_ref, second_ref, send_ref, table_ref):
         positions = rows * cols
         parts = []
         for u in range(rows // per_out):
@@ -182,52 +182,95 @@
         product_normed = normalised(product).astype(BF16)
         after = (start_ref[...] + gate_ref[...] * dot(product_normed, tri_out_ref[...])).astype(BF16)
         after_ref[...] = after
-        second_wide = normalised(after.astype(F32))
-        second = second_wide.astype(BF16)
-        width = HEADS * HEAD_DIM
-        spare = 3 * HEAD_DIM
+        second = normalised(after.astype(F32))
+        second_ref[...] = second.astype(BF16)
         lane = lane_index(8)
         for t in range(tiles):
             low = t * per_tile * cols
-            piece = second_wide[low : min(low + LANES, positions)]
+            piece = second[low : min(low + LANES, positions)]
             if piece.shape[0] < LANES:
                 piece = jnp.concatenate([piece, jnp.zeros((LANES - piece.shape[0], LANES), F32)], axis=0)
             found = dot_t(bias_ref[...], piece.astype(BF16))
             for a in range(t * per_tile, min((t + 1) * per_tile, rows)):
-                moved = roll(found, spare - (a % per_tile) * cols)
-                table_ref[pl.ds(a, 8, stride=rows), :] = jnp.where((lane >= spare) & (lane < spare + cols), moved, 0.0)
+                moved = roll(found, -(a % per_tile) * cols)
+                table_ref[pl.ds(a, 8, stride=rows), :] = jnp.where(lane < cols, moved, 0.0)
+        mixed = table_ref[:rows, :]
+        for h in range(1, HEADS):
+            mixed = mixed + roll(table_ref[h * rows : (h + 1) * rows, :], h * HEAD_DIM)
+        mixed = mixed.astype(BF16)
+        for r in range(copies):
+            send_ref[r] = mixed
+
+    return after
+
+
+def items_kernel(positions):
+    def items(second_ref, weights_ref, query_ref, items_ref, gating_ref):
+        second = second_ref[...]
         lane = lane_index(positions)
         for h in range(HEADS):
             mixed = dot(second, weights_ref[:, h * LANES : (h + 1) * LANES])
             mixed = jnp.where(lane < HEAD_DIM, mixed * HEAD_DIM ** (-0.5), mixed)
-            bias = table_ref[h * rows : (h + 1) * rows, :]
-            for group in range(rows // items):
-                low = group * items * cols
-                at = h * positions + low
-                items_ref[at : at + items * cols, :] = jnp.concatenate(
-                    [mixed[low : low + rows] + bias, mixed[low + rows : low + items * cols]], axis=0
-                ).astype(BF16)
-        gating_ref[...] = sigmoid(dot(second, query_ref[:, width:]))
-
-    return middle
-
-
-def table_kernel(rows, cols, blocks, copies):
-    def table(whole_ref, send_ref):
-        spare = 3 * HEAD_DIM
-        lane = lane_index(rows)
-        wide = blocks * cols // LANES
-        parts = [jnp.zeros((rows, LANES), F32) for _ in range(wide)]
+            items_ref[h * positions : (h + 1) * positions, :] = mixed.astype(BF16)
+        gating_ref[...] = sigmoid(dot(second, query_ref[:, HEADS * HEAD_DIM :]))
+
+    return items
+
+
+def pack_kernel(chunk, cols, length, nsub):
+    part = length // nsub
+    rest = part - chunk
+    spare = 3 * HEAD_DIM
+    thin = HEAD_DIM - cols
+
+    def pack(items_ref, table_ref, out_ref):
+        lane = lane_index(chunk)
+        thin_lane = lane_index(rest)
+        for h in range(HEADS):
+            extras = []
+            for s in range(nsub):
+                wide = table_ref[s * part : s * part + chunk, :].astype(F32)
+                wide = jnp.where((lane >= spare) & (lane < spare + cols), roll(wide, spare - h * HEAD_DIM), 0.0)
+                last = table_ref[s * part + chunk : (s + 1) * part, :].astype(F32)
+                pieces = []
+                for p in range(chunk // rest):
+                    moved = roll(last, spare + cols - h * HEAD_DIM - p * thin)
+                    pieces.append(jnp.where(thin_lane >= spare + cols, moved, 0.0))
+                extras.append(wide + jnp.concatenate(pieces, axis=0))
+            for group in range(HEADS):
+                at = (h * HEADS + group) * chunk
+                out_ref[at : at + chunk, :] = (items_ref[at : at + chunk, :].astype(F32) + extras[group % nsub]).astype(BF16)
+
+    return pack
+
+
+def table_kernel(chunk, cols, blocks, length, nsub):
+    part = length // nsub
+    rest = part - chunk
+    spare = 3 * HEAD_DIM
+    thin = HEAD_DIM - cols
+    wide = length // LANES
+
+    def table(whole_ref, out_ref):
+        lane = lane_index(chunk)
+        thin_lane = lane_index(rest)
+        upper = [jnp.zeros((chunk, LANES), F32) for _ in range(wide)]
+        lower = [jnp.zeros((rest, LANES), F32) for _ in range(wide)]
         for m in range(blocks):
-            piece = whole_ref[m, :rows, :].astype(F32)
+            piece = whole_ref[m].astype(F32)
             moved = roll(piece, m * cols - spare)
             for w in range(wide):
                 low, high = max(m * cols - w * LANES, 0), min((m + 1) * cols - w * LANES, LANES)
                 if low < high:
-                    parts[w] = jnp.where((lane >= low) & (lane < high), moved, parts[w])
-        whole = jnp.concatenate(parts, axis=1).astype(BF16)
-        for r in range(copies):
-            send_ref[r] = whole
+                    upper[w] = jnp.where((lane >= low) & (lane < high), moved, upper[w])
+            for p in range(chunk // rest):
+                at = m * cols + p * thin
+                moved = roll(piece[p * rest : (p + 1) * rest], at - spare - cols)
+                w, low = at // LANES, at % LANES
+                lower[w] = jnp.where((thin_lane >= low) & (thin_lane < low + thin), moved, lower[w])
+        for w in range(wide):
+            out_ref[:chunk, w * LANES : (w + 1) * LANES] = upper[w].astype(BF16)
+            out_ref[chunk:, w * LANES : (w + 1) * LANES] = lower[w].astype(BF16)
 
     return table
 
@@ -300,6 +343,7 @@
         common + (tri_gate, att_query, att_kv),
         "vsssvvvv",
     )
+    live, start = lax.optimization_barrier((residue_mask.astype(F32).reshape(1, length), start))
     gathered = lax.all_gather(moved.reshape(channels, 2 * tiles * LANES), "sub", axis=0, tiled=True)
     (products,) = call(
         product_kernel(rows, cols, nrow, ncol, nsub, per_tile, tiles),
@@ -313,23 +357,35 @@
     )
     returned = lax.all_to_all(products.reshape(nrow * ncol, 2, rows // 8 * LANES), ("col", "row"), split_axis=0, concat_axis=0, tiled=True)
     bias_rows = jnp.pad(att_bias.T, ((0, 8 - HEADS), (0, 0)))
-    after, gating, sent_items = call(
-        middle_kernel(rows, cols, items, per_tile, tiles),
-        [((positions, channels), BF16), ((positions, channels), F32), ((HEADS * positions, LANES), BF16)],
-        (returned.reshape(channels, rows // 4 * LANES), start, tri_gating, tri_out, head_weights, att_query, bias_rows),
-        "vvvvvvv",
+    after, second, copies = call(
+        after_kernel(rows, cols, nrow, per_tile, tiles),
+        [((positions, channels), BF16), ((positions, channels), BF16), ((nrow, rows, LANES), BF16)],
+        (returned.reshape(channels, rows // 4 * LANES), start, tri_gating, tri_out, bias_rows),
+        "vvvvv",
         scratch=[pltpu.VMEM((8 * rows, LANES), F32)],
     )
-    whole = lax.all_to_all(
-        sent_items.reshape(blocks, items * cols, LANES), ("col", "sub"), split_axis=0, concat_axis=0, tiled=True
-    )
-    (copies,) = call(table_kernel(rows, cols, blocks, nrow), [((nrow, rows, length), BF16)], (whole,), "v")
-    head_table = lax.all_to_all(copies, "row", split_axis=0, concat_axis=0, tiled=True).reshape(length, length)
+    columns = lax.all_to_all(copies, "row", split_axis=0, concat_axis=0, tiled=True)
+    plain_items, gating = call(
+        items_kernel(positions),
+        [((HEADS * positions, LANES), BF16), ((positions, channels), F32)],
+        (second, head_weights, att_query),
+        "vvv",
+    )
+    chunk = items * cols
+    (sent_items,) = call(
+        pack_kernel(chunk, cols, length, nsub),
+        [((HEADS * positions, LANES), BF16)],
+        (plain_items, columns.reshape(length, LANES)),
+        "vv",
+    )
+    whole = lax.all_to_all(sent_items.reshape(blocks, chunk, LANES), ("col", "sub"), split_axis=0, concat_axis=0, tiled=True)
+    (table_part,) = call(table_kernel(chunk, cols, blocks, length, nsub), [((length // nsub, length), BF16)], (whole,), "v")
+    head_table = lax.all_gather(table_part, "sub", axis=0, tiled=True)
     slabs = -(-items // 4)
     (attended,) = call(
         attend_kernel(items, cols, blocks),
         [((blocks, slabs * cols, LANES), BF16)],
-        (whole, head_table, residue_mask.astype(F32).reshape(1, length)),
+        (whole, head_table, live),
         "vvv",
         scratch=[pltpu.VMEM((slabs, length, LANES), F32)],
     )

time: 183 us -> 178 us (0.973)
  waiting for transfers between devices: 31 us -> 26.4 us
    all_to_all x1, waiting for transfers between devices: 15.9 us -> 11.3 us  [on_device(): lax.all_to_all(copies, 'row', split_axis=0, concat_axis=0, tiled=True)]
    all_to_all x1, blocking collectives: 16.9 us -> 13.2 us  [on_device(): lax.all_to_all(attended, ('col', 'sub'), split_axis=0, concat_axis=0, til...]
    all_gather x0 -> x1, blocking collectives: none -> 2.07 us  [on_device(): head_table = lax.all_gather(table_part, 'sub', axis=0, tiled=True)]
    pallas_call x7 -> x9, Pallas kernels: 8.79 us -> 9.49 us  [call(): pl.pallas_call(kernel, out_shape=[jax.ShapeDtypeStruct(s, t) for s, t in...]
where the time goes in v3:
time: 178 us; the launch traced here: 177 us
  blocking collectives  122 us (69%)
  waiting for transfers between devices  26.4 us (15%)
  starting transfers between devices  14.8 us (8%)
  Pallas kernels  9.49 us (5%)
  local copies, waits for them, and re-layouts  4.81 us (3%)
    all_to_all x1, blocking collectives, on_device(): lax.all_to_all(send.reshape(channels, 2, tiles * LANES), ('col', 'row'),...  76.1 us
    all_to_all x1, blocking collectives, on_device(): lax.all_to_all(sent_items.reshape(blocks, chunk, LANES), ('col', 'sub'),...  24.6 us
    all_to_all x1, waiting for transfers between devices, on_device(): lax.all_to_all(products.reshape(nrow * ncol, 2, rows // 8 * LANES), ('col...  15.1 us
    all_to_all x1, blocking collectives, on_device(): lax.all_to_all(attended, ('col', 'sub'), split_axis=0, concat_axis=0, til...  13.2 us
    all_to_all x1, waiting for transfers between devices, on_device(): lax.all_to_all(copies, 'row', split_axis=0, concat_axis=0, tiled=True)  11.3 us
    all_to_all x1, starting transfers between devices, on_device(): lax.all_to_all(products.reshape(nrow * ncol, 2, rows // 8 * LANES), ('col...  10.1 us
    pallas_call x9, Pallas kernels, call(): pl.pallas_call(kernel, out_shape=[jax.ShapeDtypeStruct(s, t) for s, t in...  9.49 us
    all_gather x1, blocking collectives, on_device(): lax.all_gather(moved.reshape(channels, 2 * tiles * LANES), 'sub', axis=0,...  5.64 us
  transfers between devices with their start and end apart: 2, of which 2 were waited for; matrix products, arithmetic and copies ran while one was open for 0% of the time, Pallas kernels for 1%

profile of v3, /device:TPU:65, one launch (start us, length us, event | category | flops | bytes accessed | tf_op | source)
XLA Modules:
  0.0 177.5 jit_solution(11368759379857674951)
XLA Ops:
  0.0 0.0 copy-start.9
  0.0 0.1 pad_add_fusion.place_ref
  0.1 0.0 copy-start.8
  0.1 0.0 copy-start.10
  0.1 0.6 copy-done.9
  0.7 0.1 copy-done.8
  0.8 0.0 copy-done.10
  0.8 0.0 copy-start
  0.8 0.9 copy-done
  1.7 0.0 copy-start.3
  1.7 0.9 copy-done.3
  2.6 1.3 sides.1
  3.9 0.1 reshape.32
  4.0 76.1 %all_to_all.25 = bf16[128,2,640]{2,1,0:T(2,128)(2,1)S(1)} all-to-all(bf16[128,2,640]{2,1,0:T(2,128)(2,1)S(1)} %reshape.32), channel_id=1, replica_groups=mesh['grp'=2,'row'=16,'col'=8,'sub'=2] {'col','row'}, dimensions={0} | all-to-all | bytes 655360 | tf_op jit(solution)/shard_map/all_to_all | solution.py:339
  80.1 5.6 %all_gather.6.gathered_ref = bf16[256,1280]{1,0:T(8,128)(2,1)S(1)} all-gather(bf16[128,1280]{1,0:T(8,128)(2,1)S(1)} %bitcast.21), channel_id=1, replica_groups=mesh['grp'=2,'row'=16,'col'=8,'sub'=2] {'sub'}, dimensions={0}, use_global_device_ids=true | all-gather | bytes 983040 | tf_op jit(solution)/shard_map/all_gather | solution.py:347
  85.8 1.8 %products.1 = bf16[128,768]{1,0:T(8,128)(2,1)S(1)} custom-call(s32[3]{0:T(128)S(1)} %pad_add_fusion.place_ref, bf16[256,1280]{1,0:T(8,128)(2,1)S(1)} %all_gather.6.gathered_ref), custom_call_target="tpu_custom_call" | custom-call | flops 4194304 | bytes 1048576 | tf_op jit(solution)/shard_map/products/pallas_call | solution.py:49
  87.6 0.7 reshape.34
  88.3 0.0 copy-start.1
  88.3 0.0 copy-start.2
  88.3 0.0 copy-start.4
  88.3 0.0 copy-start.5
  88.3 10.1 %all-to-all-start.1 = ((bf16[128,2,384]{2,1,0:T(2,128)(2,1)}), bf16[128,2,384]{2,1,0:T(2,128)(2,1)S(1)}, u32[]{:S(2)}, u32[]{:S(2)}) async-start(bf16[128,2,384]{2,1,0:T(2,128)(2,1)} %reshape.34), calls=%async_computation.1 | async-start | bytes 393216 | tf_op jit(solution)/shard_map/all_to_all | solution.py:358
  98.4 0.0 copy-done.1
  98.4 0.0 copy-done.2
  98.4 0.0 copy-done.4
  98.4 0.0 copy-done.5
  98.4 1.0 gates.1
  99.4 0.0 copy-start.11
  99.5 0.7 copy-done.11
  100.1 15.1 %all-to-all-done.1 = bf16[128,2,384]{2,1,0:T(2,128)(2,1)S(1)} async-done(((bf16[128,2,384]{2,1,0:T(2,128)(2,1)}), bf16[128,2,384]{2,1,0:T(2,128)(2,1)S(1)}, u32[]{:S(2)}, u32[]{:S(2)}) %all-to-all-start.1) | async-done | bytes 196640 | tf_op jit(solution)/shard_map/all_to_all | solution.py:358
  115.2 0.0 copy-start.6
  115.3 0.7 copy-done.6
  116.0 1.7 after.1
  117.7 4.8 %all-to-all-start.2 = ((bf16[16,24,128]{2,1,0:T(8,128)(2,1)}), bf16[16,24,128]{2,1,0:T(8,128)(2,1)S(1)}, u32[]{:S(2)}, u32[]{:S(2)}) async-start(bf16[16,24,128]{2,1,0:T(8,128)(2,1)} %get-tuple-element.21), calls=%async_computation.2 | async-start | bytes 196608 | tf_op jit(solution)/shard_map/all_to_all | solution.py:367
  122.5 0.4 items.1
  122.8 11.3 %all-to-all-done.2 = bf16[16,24,128]{2,1,0:T(8,128)(2,1)S(1)} async-done(((bf16[16,24,128]{2,1,0:T(8,128)(2,1)}), bf16[16,24,128]{2,1,0:T(8,128)(2,1)S(1)}, u32[]{:S(2)}, u32[]{:S(2)}) %all-to-all-start.2) | async-done | bytes 98336 | tf_op jit(solution)/shard_map/all_to_all | solution.py:367
  134.2 0.3 pack.1
  134.5 24.6 %all_to_all.26.whole_ref = bf16[16,144,128]{2,1,0:T(8,128)(2,1)S(1)} all-to-all(bf16[16,144,128]{2,1,0:T(8,128)(2,1)S(1)} %bitcast.13), channel_id=1, replica_groups=mesh['grp'=2,'row'=16,'col'=8,'sub'=2] {'col','sub'}, dimensions={0} | all-to-all | bytes 1179648 | tf_op jit(solution)/shard_map/all_to_all | solution.py:381
  159.1 0.4 table.1
  159.4 2.1 %all_gather.7.bias_ref = bf16[384,384]{1,0:T(8,128)(2,1)S(1)} all-gather(bf16[192,384]{1,0:T(8,128)(2,1)S(1)} %table.1), channel_id=1, replica_groups=mesh['grp'=2,'row'=16,'col'=8,'sub'=2] {'sub'}, dimensions={0}, use_global_device_ids=true | all-gather | bytes 442368 | tf_op jit(solution)/shard_map/all_gather | solution.py:383
  161.5 1.8 attend.1
  163.3 0.0 copy-start.7
  163.3 13.2 %all_to_all.27.back_ref = bf16[16,48,128]{2,1,0:T(8,128)(2,1)S(1)} all-to-all(bf16[16,48,128]{2,1,0:T(8,128)(2,1)S(1)} %attend.1), channel_id=1, replica_groups=mesh['grp'=2,'row'=16,'col'=8,'sub'=2] {'col','sub'}, dimensions={0} | all-to-all | bytes 393216 | tf_op jit(solution)/shard_map/all_to_all | solution.py:392
  176.5 0.0 copy-done.7
  176.5 1.0 finish.1
  (5 shorter events, 0.1 us)
Async XLA Ops:
  0.0 0.7 copy-start.9
  0.1 0.7 copy-start.8
  0.1 0.7 copy-start.10
  0.8 0.9 copy-start
  1.7 0.9 copy-start.3
  88.3 10.1 %copy-start.1 = (bf16[24,24,128]{2,1,0:T(8,128)(2,1)S(1)}, bf16[24,24,128]{2,1,0:T(8,128)(2,1)}, u32[]{:S(2)}) copy-start(bf16[24,24,128]{2,1,0:T(8,128)(2,1)} %param.11) | copy-start | bytes 442372
  88.3 10.1 %copy-start.2 = (bf16[128,256]{1,0:T(8,128)(2,1)S(1)}, bf16[128,256]{1,0:T(8,128)(2,1)}, u32[]{:S(2)}) copy-start(bf16[128,256]{1,0:T(8,128)(2,1)} %query_ref.3) | copy-start | bytes 196612
  88.3 10.1 %copy-start.4 = (bf16[128,256]{1,0:T(8,128)(2,1)S(1)}, bf16[128,256]{1,0:T(8,128)(2,1)}, u32[]{:S(2)}) copy-start(bf16[128,256]{1,0:T(8,128)(2,1)} %keyval_ref.1) | copy-start | bytes 196612
  88.3 10.1 %copy-start.5 = (bf16[128,128]{1,0:T(8,128)(2,1)S(1)}, bf16[128,128]{1,0:T(8,128)(2,1)}, u32[]{:S(2)}) copy-start(bf16[128,128]{1,0:T(8,128)(2,1)} %tri_gate_ref.1) | copy-start | bytes 98308
  88.3 26.9 %all-to-all-start.1 = ((bf16[128,2,384]{2,1,0:T(2,128)(2,1)}), bf16[128,2,384]{2,1,0:T(2,128)(2,1)S(1)}, u32[]{:S(2)}, u32[]{:S(2)}) async-start(bf16[128,2,384]{2,1,0:T(2,128)(2,1)} %reshape.34), calls=%async_computation.1 | async-start | bytes 393216 | tf_op jit(solution)/shard_map/all_to_all | solution.py:358
  99.4 0.7 copy-start.11
  115.2 0.8 copy-start.6
  117.7 16.5 %all-to-all-start.2 = ((bf16[16,24,128]{2,1,0:T(8,128)(2,1)}), bf16[16,24,128]{2,1,0:T(8,128)(2,1)S(1)}, u32[]{:S(2)}, u32[]{:S(2)}) async-start(bf16[16,24,128]{2,1,0:T(8,128)(2,1)} %get-tuple-element.21), calls=%async_computation.2 | async-start | bytes 196608 | tf_op jit(solution)/shard_map/all_to_all | solution.py:367
  163.3 13.2 %copy-start.7 = (bf16[128,128]{1,0:T(8,128)(2,1)S(1)}, bf16[128,128]{1,0:T(8,128)(2,1)}, u32[]{:S(2)}) copy-start(bf16[128,128]{1,0:T(8,128)(2,1)} %att_out_ref.1) | copy-start | bytes 98308

commit v4 on v3

--- a/solution.py
+++ b/solution.py
@@ -43,13 +43,18 @@
     return values if shift == 0 else pltpu.roll(values, shift, 1)
 
 
+def in_hbm(values):
+    return values if INTERPRET else pltpu.with_memory_space_constraint(values, pltpu.HBM)
+
+
 def call(kernel, outs, ins, spaces, scratch=(), flops=1 << 22):
     vmem = pl.BlockSpec(memory_space=pltpu.VMEM)
     smem = pl.BlockSpec(memory_space=pltpu.SMEM)
+    hbm = pl.BlockSpec(memory_space=pltpu.HBM)
     return pl.pallas_call(
         kernel,
         out_shape=[jax.ShapeDtypeStruct(s, t) for s, t in outs],
-        in_specs=[smem if k == "s" else vmem for k in spaces],
+        in_specs=[{"s": smem, "v": vmem, "h": hbm}[k] for k in spaces],
         out_specs=[vmem] * len(outs),
         scratch_shapes=list(scratch),
         interpret=INTERPRET,
@@ -79,7 +84,14 @@
 
 
 def sides_kernel(rows, cols, per_tile, tiles):
-    def sides(pair_ref, chain_ref, live_ref, place_ref, vec_ref, tri_in_ref, send_ref):
+    def sides(place_ref, *refs):
+        outside, send_ref, inside, sems = refs[:5], refs[5], refs[6:11], refs[11:]
+        copies = [pltpu.make_async_copy(a, b, c) for a, b, c in zip(outside, inside, sems)]
+        for copy in copies:
+            copy.start()
+        for copy in copies:
+            copy.wait()
+        pair_ref, chain_ref, live_ref, vec_ref, tri_in_ref = inside
         start, mask = start_block(pair_ref, chain_ref, live_ref, place_ref, vec_ref, rows, cols)
         normed = normalised(start).astype(BF16).astype(F32) * mask
         weights = tri_in_ref[...].astype(F32).T.astype(BF16)
@@ -99,7 +111,7 @@
 
 
 def gate_kernel(rows, cols):
-    def gates(pair_ref, chain_ref, live_ref, place_ref, vec_ref, tri_gate_ref, query_ref, keyval_ref, start_ref, gate_ref, weights_ref):
+    def gates(pair_ref, chain_ref, live_ref, place_ref, vec_ref, tri_gate_ref, query_ref, keyval_ref, tri_out_ref, bias_ref, start_ref, gate_ref, weights_ref, out_ref, wide_ref):
         start, _ = start_block(pair_ref, chain_ref, live_ref, place_ref, vec_ref, rows, cols)
         start_ref[...] = start
         gate_ref[...] = sigmoid(dot(normalised(start).astype(BF16), tri_gate_ref[...]))
@@ -114,6 +126,13 @@
             mixed = jnp.where(lane < 2 * HEAD_DIM, mixed, roll(values, 2 * HEAD_DIM - low))
             mixed = jnp.where(lane < 3 * HEAD_DIM, mixed, 0.0)
             weights_ref[:, h * LANES : (h + 1) * LANES] = mixed.astype(BF16)
+        out_ref[...] = tri_out_ref[...]
+        bias = jnp.concatenate([bias_ref[...].astype(F32), jnp.zeros((LANES - 8, LANES), F32)], axis=0).T
+        mixed = jnp.zeros(bias.shape, F32)
+        for h in range(HEADS):
+            inside = (lane >= h * HEAD_DIM) & (lane < h * HEAD_DIM + cols)
+            mixed = jnp.where(inside, bias[:, h : h + 1], mixed)
+        wide_ref[...] = mixed.astype(BF16)
 
     return gates
 
@@ -170,10 +189,10 @@
     return products
 
 
-def after_kernel(rows, cols, copies, per_tile, tiles):
+def after_kernel(rows, cols, copies):
     per_out = 4
 
-    def after(back_ref, start_ref, gate_ref, tri_out_ref, bias_ref, after_ref, second_ref, send_ref, table_ref):
+    def after(back_ref, start_ref, gate_ref, tri_out_ref, bias_ref, after_ref, second_ref, send_ref):
         positions = rows * cols
         parts = []
         for u in range(rows // per_out):
@@ -182,22 +201,16 @@
         product_normed = normalised(product).astype(BF16)
         after = (start_ref[...] + gate_ref[...] * dot(product_normed, tri_out_ref[...])).astype(BF16)
         after_ref[...] = after
-        second = normalised(after.astype(F32))
-        second_ref[...] = second.astype(BF16)
-        lane = lane_index(8)
-        for t in range(tiles):
-            low = t * per_tile * cols
-            piece = second[low : min(low + LANES, positions)]
-            if piece.shape[0] < LANES:
-                piece = jnp.concatenate([piece, jnp.zeros((LANES - piece.shape[0], LANES), F32)], axis=0)
-            found = dot_t(bias_ref[...], piece.astype(BF16))
-            for a in range(t * per_tile, min((t + 1) * per_tile, rows)):
-                moved = roll(found, -(a % per_tile) * cols)
-                table_ref[pl.ds(a, 8, stride=rows), :] = jnp.where(lane < cols, moved, 0.0)
-        mixed = table_ref[:rows, :]
-        for h in range(1, HEADS):
-            mixed = mixed + roll(table_ref[h * rows : (h + 1) * rows, :], h * HEAD_DIM)
-        mixed = mixed.astype(BF16)
+        second = normalised(after.astype(F32)).astype(BF16)
+        second_ref[...] = second
+        found = dot(second, bias_ref[...])
+        own = lax.broadcasted_iota(jnp.int32, (cols, LANES), 0) == lane_index(cols) % HEAD_DIM
+        found = [jnp.where(own, found[a * cols : (a + 1) * cols], 0.0) for a in range(rows)]
+        found = jnp.concatenate(found, axis=0).astype(BF16)
+        at = lax.broadcasted_iota(jnp.int32, (rows, positions), 0) * cols
+        spot = lax.broadcasted_iota(jnp.int32, (rows, positions), 1)
+        mine = jnp.where((spot >= at) & (spot < at + cols), 1.0, 0.0).astype(BF16)
+        mixed = dot(mine, found).astype(BF16)
         for r in range(copies):
             send_ref[r] = mixed
 
@@ -277,30 +290,49 @@
 
 def attend_kernel(items, cols, blocks):
     length = blocks * cols
-
-    def attend(whole_ref, bias_ref, live_ref, send_ref, slab_ref):
-        bias = bias_ref[...].astype(F32)
-        live = live_ref[...]
+    full = items // 4 * 4
+    whole_rows = 16
+
+    def attend(whole_ref, bias_ref, live_ref, send_ref):
+        bias = jnp.where(live_ref[...] > 0.0, bias_ref[...].astype(F32), -jnp.inf)
         lane = lane_index(length)
-        slab_ref[...] = jnp.zeros(slab_ref.shape, F32)
+        slab = jnp.zeros((length, LANES), F32)
         for a in range(items):
             piece = jnp.concatenate([whole_ref[m, a * cols : (a + 1) * cols, :].astype(F32) for m in range(blocks)], axis=0)
             query = piece[:, :HEAD_DIM].astype(BF16)
             keys = piece[:, HEAD_DIM : 2 * HEAD_DIM].astype(BF16)
-            weights = (jnp.exp(dot_t(query, keys) + bias) * live).astype(BF16)
+            weights = jnp.exp(dot_t(query, keys) + bias).astype(BF16)
             summed = dot(weights, jnp.where(lane < 3 * HEAD_DIM, piece, 1.0).astype(BF16))
             ratio = summed / roll(summed, -HEAD_DIM)
             group = a % 4
             inside = (lane >= group * HEAD_DIM) & (lane < (group + 1) * HEAD_DIM)
-            slab_ref[a // 4] = jnp.where(inside, roll(ratio, (group - 2) * HEAD_DIM), slab_ref[a // 4])
-        for part in range(slab_ref.shape[0]):
-            for m in range(blocks):
-                send_ref[m, part * cols : (part + 1) * cols, :] = slab_ref[part, m * cols : (m + 1) * cols, :].astype(BF16)
+            slab = jnp.where(inside, roll(ratio, (group - 2) * HEAD_DIM), slab)
+            if a == full - 1:
+                for m in range(blocks):
+                    send_ref[m, :cols, :] = slab[m * cols : (m + 1) * cols].astype(BF16)
+                slab = jnp.zeros((length, LANES), F32)
+        moved = roll(slab, 2 * HEAD_DIM)
+        moved_on = roll(slab, HEAD_DIM)
+        lane = lane_index(8)
+        third = (lane >= 2 * HEAD_DIM) & (lane < 3 * HEAD_DIM)
+        for m in range(blocks):
+            low = m * cols
+            tail = low + whole_rows
+            out = jnp.concatenate(
+                [
+                    jnp.where(third, moved[tail : tail + 8], slab[low : low + 8]),
+                    jnp.where(third, moved_on[tail : tail + 8], slab[low + 8 : tail]),
+                ],
+                axis=0,
+            )
+            send_ref[m, cols:, :] = out.astype(BF16)
 
     return attend
 
 
 def finish_kernel(rows, cols, items):
+    whole_rows = 16
+
     def finish(back_ref, gating_ref, after_ref, att_out_ref, out_ref):
         lane = lane_index(cols)
         pieces = []
@@ -308,9 +340,17 @@
             group, item = a // items, a % items
             mixed = jnp.zeros((cols, LANES), F32)
             for h in range(HEADS):
-                part = back_ref[h * (rows // items) + group, (item // 4) * cols : (item // 4 + 1) * cols, :].astype(F32)
+                block = h * (rows // items) + group
+                if item < 4:
+                    part = roll(back_ref[block, :cols, :].astype(F32), (h - item) * HEAD_DIM)
+                else:
+                    late = back_ref[block, cols:, :].astype(F32)
+                    last = late[(item - 4) * 8 : (item - 3) * 8]
+                    part = jnp.concatenate(
+                        [roll(late, (h - item + 4) * HEAD_DIM), roll(last, (h - 2) * HEAD_DIM)], axis=0
+                    )
                 inside = (lane >= h * HEAD_DIM) & (lane < (h + 1) * HEAD_DIM)
-                mixed = jnp.where(inside, roll(part, (h - item % 4) * HEAD_DIM), mixed)
+                mixed = jnp.where(inside, part, mixed)
             pieces.append(mixed)
         attended = jnp.concatenate(pieces, axis=0)
         outgoing = (attended * gating_ref[...]).astype(BF16)
@@ -335,13 +375,33 @@
     vec = chain_vec.reshape(1, channels)
     common = (flat, chain_ids, residue_mask, place, vec)
 
-    (send,) = call(sides_kernel(rows, cols, per_tile, tiles), [((channels, 2 * tiles * LANES), BF16)], common + (tri_in,), "vsssvv")
+    (send,) = call(
+        sides_kernel(rows, cols, per_tile, tiles),
+        [((channels, 2 * tiles * LANES), BF16)],
+        (place,) + tuple(in_hbm(x) for x in (flat, chain_ids, residue_mask, vec, tri_in)),
+        "shhhhh",
+        scratch=[
+            pltpu.VMEM(flat.shape, flat.dtype),
+            pltpu.SMEM(chain_ids.shape, jnp.int32),
+            pltpu.SMEM(residue_mask.shape, jnp.int32),
+            pltpu.VMEM(vec.shape, F32),
+            pltpu.VMEM(tri_in.shape, tri_in.dtype),
+        ]
+        + [pltpu.SemaphoreType.DMA] * 5,
+    )
     moved = lax.all_to_all(send.reshape(channels, 2, tiles * LANES), ("col", "row"), split_axis=0, concat_axis=0, tiled=True)
-    start, tri_gating, head_weights = call(
+    bias_rows = jnp.pad(att_bias.T, ((0, 8 - HEADS), (0, 0)))
+    start, tri_gating, head_weights, near_out, wide_bias = call(
         gate_kernel(rows, cols),
-        [((positions, channels), F32), ((positions, channels), F32), ((channels, HEADS * LANES), BF16)],
-        common + (tri_gate, att_query, att_kv),
-        "vsssvvvv",
+        [
+            ((positions, channels), F32),
+            ((positions, channels), F32),
+            ((channels, HEADS * LANES), BF16),
+            (tri_out.shape, BF16),
+            ((channels, LANES), BF16),
+        ],
+        common + (tri_gate, att_query, att_kv, tri_out, bias_rows),
+        "vsssvvvvvv",
     )
     live, start = lax.optimization_barrier((residue_mask.astype(F32).reshape(1, length), start))
     gathered = lax.all_gather(moved.reshape(channels, 2 * tiles * LANES), "sub", axis=0, tiled=True)
@@ -356,13 +416,11 @@
         ],
     )
     returned = lax.all_to_all(products.reshape(nrow * ncol, 2, rows // 8 * LANES), ("col", "row"), split_axis=0, concat_axis=0, tiled=True)
-    bias_rows = jnp.pad(att_bias.T, ((0, 8 - HEADS), (0, 0)))
     after, second, copies = call(
-        after_kernel(rows, cols, nrow, per_tile, tiles),
+        after_kernel(rows, cols, nrow),
         [((positions, channels), BF16), ((positions, channels), BF16), ((nrow, rows, LANES), BF16)],
-        (returned.reshape(channels, rows // 4 * LANES), start, tri_gating, tri_out, bias_rows),
+        (returned.reshape(channels, rows // 4 * LANES), start, tri_gating, near_out, wide_bias),
         "vvvvv",
-        scratch=[pltpu.VMEM((8 * rows, LANES), F32)],
     )
     columns = lax.all_to_all(copies, "row", split_axis=0, concat_axis=0, tiled=True)
     plain_items, gating = call(
@@ -381,13 +439,8 @@
     whole = lax.all_to_all(sent_items.reshape(blocks, chunk, LANES), ("col", "sub"), split_axis=0, concat_axis=0, tiled=True)
     (table_part,) = call(table_kernel(chunk, cols, blocks, length, nsub), [((length // nsub, length), BF16)], (whole,), "v")
     head_table = lax.all_gather(table_part, "sub", axis=0, tiled=True)
-    slabs = -(-items // 4)
     (attended,) = call(
-        attend_kernel(items, cols, blocks),
-        [((blocks, slabs * cols, LANES), BF16)],
-        (whole, head_table, live),
-        "vvv",
-        scratch=[pltpu.VMEM((slabs, length, LANES), F32)],
+        attend_kernel(items, cols, blocks), [((blocks, cols + 16, LANES), BF16)], (whole, head_table, live), "vvv"
     )
     back = lax.all_to_all(attended, ("col", "sub"), split_axis=0, concat_axis=0, tiled=True)
     (result,) = call(

time: 178 us -> 175 us (0.983)
  local copies, waits for them, and re-layouts: 4.81 us -> 2.21 us
    unnamed x26 -> x22, local copies, waits for them, and re-layouts: 3.99 us -> 1.39 us
where the time goes in v4:
time: 175 us
  blocking collectives  121 us (69%)
  waiting for transfers between devices  25.7 us (15%)
  starting transfers between devices  14.8 us (8%)
  Pallas kernels  10.5 us (6%)
  local copies, waits for them, and re-layouts  2.21 us (1%)
    all_to_all x1, blocking collectives, on_device(): lax.all_to_all(send.reshape(channels, 2, tiles * LANES), ('col', 'row'),...  76.1 us
    all_to_all x1, blocking collectives, on_device(): lax.all_to_all(sent_items.reshape(blocks, chunk, LANES), ('col', 'sub'),...  24.6 us
    all_to_all x1, waiting for transfers between devices, on_device(): lax.all_to_all(products.reshape(nrow * ncol, 2, rows // 8 * LANES), ('col...  14.4 us
    all_to_all x1, blocking collectives, on_device(): lax.all_to_all(attended, ('col', 'sub'), split_axis=0, concat_axis=0, til...  12.5 us
    all_to_all x1, waiting for transfers between devices, on_device(): lax.all_to_all(copies, 'row', split_axis=0, concat_axis=0, tiled=True)  11.3 us
    pallas_call x9, Pallas kernels, call(): pl.pallas_call(kernel, out_shape=[jax.ShapeDtypeStruct(s, t) for s, t in...  10.5 us
    all_to_all x1, starting transfers between devices, on_device(): lax.all_to_all(products.reshape(nrow * ncol, 2, rows // 8 * LANES), ('col...  10.1 us
    all_gather x1, blocking collectives, on_device(): lax.all_gather(moved.reshape(channels, 2 * tiles * LANES), 'sub', axis=0,...  5.64 us
  transfers between devices with their start and end apart: 2, of which 2 were waited for; matrix products, arithmetic and copies ran while one was open for 0% of the time, Pallas kernels for 1%

profile of v4, /device:TPU:65, one launch (start us, length us, event | category | flops | bytes accessed | tf_op | source)
XLA Modules:
  0.0 174.5 jit_solution(12549163040004515926)
XLA Ops:
  0.0 0.1 pad_add_fusion.place_ref
  0.1 2.3 %sides.1 = bf16[128,1280]{1,0:T(8,128)(2,1)S(1)} custom-call(s32[3]{0:T(128)S(1)} %pad_add_fusion.place_ref, bf16[576,128]{1,0:T(8,128)(2,1)} %bitcast.15, s32[384]{0:T(512)} %chain_ref.1, s32[384]{0:T(512)} %live_ref.1, f32[1,128]{1,0:T(1,128)} %bitcast.18, bf16[128,512]{1,0:T(8,128)(2,1)} %refs_4_.1), custom_call_target="tpu_custom_call" | custom-call | flops 4194304 | bytes 1048576 | tf_op jit(solution)/shard_map/sides/pallas_call | solution.py:54
  2.4 0.1 reshape.32
  2.5 76.1 %all_to_all.25 = bf16[128,2,640]{2,1,0:T(2,128)(2,1)S(1)} all-to-all(bf16[128,2,640]{2,1,0:T(2,128)(2,1)S(1)} %reshape.32), channel_id=1, replica_groups=mesh['grp'=2,'row'=16,'col'=8,'sub'=2] {'col','row'}, dimensions={0} | all-to-all | bytes 655360 | tf_op jit(solution)/shard_map/all_to_all | solution.py:392
  78.6 5.6 %all_gather.6.gathered_ref = bf16[256,1280]{1,0:T(8,128)(2,1)S(1)} all-gather(bf16[128,1280]{1,0:T(8,128)(2,1)S(1)} %bitcast.21), channel_id=1, replica_groups=mesh['grp'=2,'row'=16,'col'=8,'sub'=2] {'sub'}, dimensions={0}, use_global_device_ids=true | all-gather | bytes 983040 | tf_op jit(solution)/shard_map/all_gather | solution.py:407
  84.3 1.8 %products.1 = bf16[128,768]{1,0:T(8,128)(2,1)S(1)} custom-call(s32[3]{0:T(128)S(1)} %pad_add_fusion.place_ref, bf16[256,1280]{1,0:T(8,128)(2,1)S(1)} %all_gather.6.gathered_ref), custom_call_target="tpu_custom_call" | custom-call | flops 4194304 | bytes 1048576 | tf_op jit(solution)/shard_map/products/pallas_call | solution.py:54
  86.1 0.7 reshape.34
  86.8 0.0 copy-start.6
  86.8 0.0 copy-start
  86.8 0.0 copy-start.1
  86.8 0.0 copy-start.2
  86.8 0.0 copy-start.4
  86.8 0.0 copy-start.5
  86.8 10.1 %all-to-all-start.1 = ((bf16[128,2,384]{2,1,0:T(2,128)(2,1)}), bf16[128,2,384]{2,1,0:T(2,128)(2,1)S(1)}, u32[]{:S(2)}, u32[]{:S(2)}) async-start(bf16[128,2,384]{2,1,0:T(2,128)(2,1)} %reshape.34), calls=%async_computation.1 | async-start | bytes 393216 | tf_op jit(solution)/shard_map/all_to_all | solution.py:418
  96.9 0.0 copy-done.6
  96.9 0.0 copy-start.9
  96.9 0.7 copy-done.9
  97.6 0.0 copy-start.7
  97.6 0.0 copy-start.8
  97.6 0.0 copy-done
  97.6 0.0 copy-done.1
  97.6 0.0 copy-done.2
  97.6 0.0 copy-done.4
  97.7 0.0 copy-done.5
  97.7 0.6 copy-done.7
  98.3 0.0 copy-done.8
  98.3 1.0 gates.1
  99.3 14.4 %all-to-all-done.1 = bf16[128,2,384]{2,1,0:T(2,128)(2,1)S(1)} async-done(((bf16[128,2,384]{2,1,0:T(2,128)(2,1)}), bf16[128,2,384]{2,1,0:T(2,128)(2,1)S(1)}, u32[]{:S(2)}, u32[]{:S(2)}) %all-to-all-start.1) | async-done | bytes 196640 | tf_op jit(solution)/shard_map/all_to_all | solution.py:418
  113.8 1.6 after.1
  115.4 4.8 %all-to-all-start.2 = ((bf16[16,24,128]{2,1,0:T(8,128)(2,1)}), bf16[16,24,128]{2,1,0:T(8,128)(2,1)S(1)}, u32[]{:S(2)}, u32[]{:S(2)}) async-start(bf16[16,24,128]{2,1,0:T(8,128)(2,1)} %get-tuple-element.25), calls=%async_computation.2 | async-start | bytes 196608 | tf_op jit(solution)/shard_map/all_to_all | solution.py:425
  120.2 0.4 items.1
  120.5 11.3 %all-to-all-done.2 = bf16[16,24,128]{2,1,0:T(8,128)(2,1)S(1)} async-done(((bf16[16,24,128]{2,1,0:T(8,128)(2,1)}), bf16[16,24,128]{2,1,0:T(8,128)(2,1)S(1)}, u32[]{:S(2)}, u32[]{:S(2)}) %all-to-all-start.2) | async-done | bytes 98336 | tf_op jit(solution)/shard_map/all_to_all | solution.py:425
  131.9 0.3 pack.1
  132.2 24.6 %all_to_all.26.whole_ref = bf16[16,144,128]{2,1,0:T(8,128)(2,1)S(1)} all-to-all(bf16[16,144,128]{2,1,0:T(8,128)(2,1)S(1)} %bitcast.13), channel_id=1, replica_groups=mesh['grp'=2,'row'=16,'col'=8,'sub'=2] {'col','sub'}, dimensions={0} | all-to-all | bytes 1179648 | tf_op jit(solution)/shard_map/all_to_all | solution.py:439
  156.7 0.4 table.1
  157.1 2.1 %all_gather.7.bias_ref = bf16[384,384]{1,0:T(8,128)(2,1)S(1)} all-gather(bf16[192,384]{1,0:T(8,128)(2,1)S(1)} %table.1), channel_id=1, replica_groups=mesh['grp'=2,'row'=16,'col'=8,'sub'=2] {'sub'}, dimensions={0}, use_global_device_ids=true | all-gather | bytes 442368 | tf_op jit(solution)/shard_map/all_gather | solution.py:441
  159.2 1.8 %attend.1 = bf16[16,40,128]{2,1,0:T(8,128)(2,1)S(1)} custom-call(bf16[16,144,128]{2,1,0:T(8,128)(2,1)S(1)} %all_to_all.26.whole_ref, bf16[384,384]{1,0:T(8,128)(2,1)S(1)} %all_gather.7.bias_ref, f32[1,384]{1,0:T(1,128)S(1)} %reshape.36.live_ref), custom_call_target="tpu_custom_call" | custom-call | flops 4194304 | bytes 1048576 | tf_op jit(solution)/shard_map/attend/pallas_call | solution.py:54
  161.0 0.0 copy-start.3
  161.0 12.5 %all_to_all.27.back_ref = bf16[16,40,128]{2,1,0:T(8,128)(2,1)S(1)} all-to-all(bf16[16,40,128]{2,1,0:T(8,128)(2,1)S(1)} %attend.1), channel_id=1, replica_groups=mesh['grp'=2,'row'=16,'col'=8,'sub'=2] {'col','sub'}, dimensions={0} | all-to-all | bytes 327680 | tf_op jit(solution)/shard_map/all_to_all | solution.py:445
  173.5 0.0 copy-done.3
  173.5 1.0 finish.1
  (5 shorter events, 0.1 us)
Async XLA Ops:
  86.8 10.1 %copy-start.6 = (s32[384]{0:T(512)S(1)}, s32[384]{0:T(512)}, u32[]{:S(2)}) copy-start(s32[384]{0:T(512)} %live_ref.1) | copy-start | bytes 4612
  86.8 10.8 %copy-start = (bf16[24,24,128]{2,1,0:T(8,128)(2,1)S(1)}, bf16[24,24,128]{2,1,0:T(8,128)(2,1)}, u32[]{:S(2)}) copy-start(bf16[24,24,128]{2,1,0:T(8,128)(2,1)} %param.11) | copy-start | bytes 442372
  86.8 10.8 %copy-start.1 = (bf16[128,256]{1,0:T(8,128)(2,1)S(1)}, bf16[128,256]{1,0:T(8,128)(2,1)}, u32[]{:S(2)}) copy-start(bf16[128,256]{1,0:T(8,128)(2,1)} %query_ref.3) | copy-start | bytes 196612
  86.8 10.8 %copy-start.2 = (bf16[128,256]{1,0:T(8,128)(2,1)S(1)}, bf16[128,256]{1,0:T(8,128)(2,1)}, u32[]{:S(2)}) copy-start(bf16[128,256]{1,0:T(8,128)(2,1)} %keyval_ref.1) | copy-start | bytes 196612
  86.8 10.8 %copy-start.4 = (bf16[128,128]{1,0:T(8,128)(2,1)S(1)}, bf16[128,128]{1,0:T(8,128)(2,1)}, u32[]{:S(2)}) copy-start(bf16[128,128]{1,0:T(8,128)(2,1)} %tri_gate_ref.1) | copy-start | bytes 98308
  86.8 10.8 %copy-start.5 = (bf16[128,128]{1,0:T(8,128)(2,1)S(1)}, bf16[128,128]{1,0:T(8,128)(2,1)}, u32[]{:S(2)}) copy-start(bf16[128,128]{1,0:T(8,128)(2,1)} %tri_out_ref.1) | copy-start | bytes 98308
  86.8 26.9 %all-to-all-start.1 = ((bf16[128,2,384]{2,1,0:T(2,128)(2,1)}), bf16[128,2,384]{2,1,0:T(2,128)(2,1)S(1)}, u32[]{:S(2)}, u32[]{:S(2)}) async-start(bf16[128,2,384]{2,1,0:T(2,128)(2,1)} %reshape.34), calls=%async_computation.1 | async-start | bytes 393216 | tf_op jit(solution)/shard_map/all_to_all | solution.py:418
  96.9 0.7 copy-start.9
  97.6 0.7 copy-start.7
  97.6 0.7 copy-start.8
  115.4 16.5 %all-to-all-start.2 = ((bf16[16,24,128]{2,1,0:T(8,128)(2,1)}), bf16[16,24,128]{2,1,0:T(8,128)(2,1)S(1)}, u32[]{:S(2)}, u32[]{:S(2)}) async-start(bf16[16,24,128]{2,1,0:T(8,128)(2,1)} %get-tuple-element.25), calls=%async_computation.2 | async-start | bytes 196608 | tf_op jit(solution)/shard_map/all_to_all | solution.py:425
  161.0 12.5 %copy-start.3 = (bf16[128,128]{1,0:T(8,128)(2,1)S(1)}, bf16[128,128]{1,0:T(8,128)(2,1)}, u32[]{:S(2)}) copy-start(bf16[128,128]{1,0:T(8,128)(2,1)} %att_out_ref.1) | copy-start | bytes 98308

commit v5 on v4

--- a/solution.py
+++ b/solution.py
@@ -169,7 +169,7 @@
             for g in range(groups):
                 parts = []
                 for q in range(ncol // 2):
-                    at = ((half * (ncol // 2) + q) * nsub + sub) * rows
+                    at = (((half * (ncol // 2) + q) * nsub + sub) * (nrow // 2 - 1) % nrow) * rows
                     parts.append(right_ref[pl.ds(pl.multiple_of(g * length + at, 8), rows), :])
                 parts.append(jnp.zeros((LANES - rows * (ncol // 2), LANES), F32))
                 chosen.append(jnp.concatenate(parts, axis=0))
@@ -359,11 +359,17 @@
     return finish
 
 
+def member_order(nrow, ncol):
+    step = nrow // 2 - 1
+    return [[c * nrow + step * p % nrow for c in range(ncol) for p in range(nrow)]]
+
+
 def on_device(
     pair, chain_ids, residue_mask, chain_vec, tri_in, tri_gate, tri_out, att_query, att_kv, att_bias, att_out
 ):
     rows, cols, channels = pair.shape
     nrow, ncol, nsub = lax.axis_size("row"), lax.axis_size("col"), lax.axis_size("sub")
+    order = member_order(nrow, ncol)
     positions = rows * cols
     length = chain_ids.shape[0]
     blocks = ncol * nsub
@@ -389,7 +395,7 @@
         ]
         + [pltpu.SemaphoreType.DMA] * 5,
     )
-    moved = lax.all_to_all(send.reshape(channels, 2, tiles * LANES), ("col", "row"), split_axis=0, concat_axis=0, tiled=True)
+    moved = lax.all_to_all(send.reshape(channels, 2, tiles * LANES), ("col", "row"), split_axis=0, concat_axis=0, tiled=True, axis_index_groups=order)
     bias_rows = jnp.pad(att_bias.T, ((0, 8 - HEADS), (0, 0)))
     start, tri_gating, head_weights, near_out, wide_bias = call(
         gate_kernel(rows, cols),
@@ -415,7 +421,7 @@
             pltpu.VMEM((blocks // 4 * length, LANES), F32),
         ],
     )
-    returned = lax.all_to_all(products.reshape(nrow * ncol, 2, rows // 8 * LANES), ("col", "row"), split_axis=0, concat_axis=0, tiled=True)
+    returned = lax.all_to_all(products.reshape(nrow * ncol, 2, rows // 8 * LANES), ("col", "row"), split_axis=0, concat_axis=0, tiled=True, axis_index_groups=order)
     after, second, copies = call(
         after_kernel(rows, cols, nrow),
         [((positions, channels), BF16), ((positions, channels), BF16), ((nrow, rows, LANES), BF16)],

time: 175 us -> 176 us (level)
  no operation moved by 1% of the time
where the time goes in v5:
time: 176 us; the launch traced here: 175 us
  blocking collectives  121 us (69%)
  waiting for transfers between devices  26.2 us (15%)
  starting transfers between devices  14.4 us (8%)
  Pallas kernels  10.5 us (6%)
  local copies, waits for them, and re-layouts  2.21 us (1%)
    all_to_all x1, blocking collectives, on_device(): lax.all_to_all(send.reshape(channels, 2, tiles * LANES), ('col', 'row'),...  76.3 us
    all_to_all x1, blocking collectives, on_device(): lax.all_to_all(sent_items.reshape(blocks, chunk, LANES), ('col', 'sub'),...  24.9 us
    all_to_all x1, waiting for transfers between devices, on_device(): lax.all_to_all(products.reshape(nrow * ncol, 2, rows // 8 * LANES), ('col...  14.9 us
    all_to_all x1, blocking collectives, on_device(): lax.all_to_all(attended, ('col', 'sub'), split_axis=0, concat_axis=0, til...  12.5 us
    all_to_all x1, waiting for transfers between devices, on_device(): lax.all_to_all(copies, 'row', split_axis=0, concat_axis=0, tiled=True)  11.3 us
    pallas_call x9, Pallas kernels, call(): pl.pallas_call(kernel, out_shape=[jax.ShapeDtypeStruct(s, t) for s, t in...  10.5 us
    all_to_all x1, starting transfers between devices, on_device(): lax.all_to_all(products.reshape(nrow * ncol, 2, rows // 8 * LANES), ('col...  10.1 us
    all_gather x1, blocking collectives, on_device(): lax.all_gather(moved.reshape(channels, 2 * tiles * LANES), 'sub', axis=0,...  5.58 us
  transfers between devices with their start and end apart: 2, of which 2 were waited for; matrix products, arithmetic and copies ran while one was open for 0% of the time, Pallas kernels for 1%

profile of v5, /device:TPU:65, one launch (start us, length us, event | category | flops | bytes accessed | tf_op | source)
XLA Modules:
  0.0 175.0 jit_solution(12407723254360166602)
XLA Ops:
  0.0 0.1 pad_add_fusion.place_ref
  0.1 2.3 %sides.1 = bf16[128,1280]{1,0:T(8,128)(2,1)S(1)} custom-call(s32[3]{0:T(128)S(1)} %pad_add_fusion.place_ref, bf16[576,128]{1,0:T(8,128)(2,1)} %bitcast.15, s32[384]{0:T(512)} %chain_ref.1, s32[384]{0:T(512)} %live_ref.1, f32[1,128]{1,0:T(1,128)} %bitcast.18, bf16[128,512]{1,0:T(8,128)(2,1)} %refs_4_.1), custom_call_target="tpu_custom_call" | custom-call | flops 4194304 | bytes 1048576 | tf_op jit(solution)/shard_map/sides/pallas_call | solution.py:54
  2.4 0.1 reshape.32
  2.5 76.3 %all_to_all.25 = bf16[128,2,640]{2,1,0:T(2,128)(2,1)S(1)} all-to-all(bf16[128,2,640]{2,1,0:T(2,128)(2,1)S(1)} %reshape.32), channel_id=1, replica_groups={{0,112,224,80,192,48,160,16,128,240,96,208,64,176,32,144,2,114,226,82,1..., dimensions={0} | all-to-all | bytes 655360 | tf_op jit(solution)/shard_map/all_to_all | solution.py:398
  78.8 5.6 %all_gather.6.gathered_ref = bf16[256,1280]{1,0:T(8,128)(2,1)S(1)} all-gather(bf16[128,1280]{1,0:T(8,128)(2,1)S(1)} %bitcast.21), channel_id=1, replica_groups=mesh['grp'=2,'row'=16,'col'=8,'sub'=2] {'sub'}, dimensions={0}, use_global_device_ids=true | all-gather | bytes 983040 | tf_op jit(solution)/shard_map/all_gather | solution.py:413
  84.4 1.8 %products.1 = bf16[128,768]{1,0:T(8,128)(2,1)S(1)} custom-call(s32[3]{0:T(128)S(1)} %pad_add_fusion.place_ref, bf16[256,1280]{1,0:T(8,128)(2,1)S(1)} %all_gather.6.gathered_ref), custom_call_target="tpu_custom_call" | custom-call | flops 4194304 | bytes 1048576 | tf_op jit(solution)/shard_map/products/pallas_call | solution.py:54
  86.2 0.7 reshape.34
  86.9 0.0 copy-start.6
  86.9 0.0 copy-start
  86.9 0.0 copy-start.1
  87.0 0.0 copy-start.2
  87.0 0.0 copy-start.4
  87.0 0.0 copy-start.5
  87.0 10.1 %all-to-all-start.1 = ((bf16[128,2,384]{2,1,0:T(2,128)(2,1)}), bf16[128,2,384]{2,1,0:T(2,128)(2,1)S(1)}, u32[]{:S(2)}, u32[]{:S(2)}) async-start(bf16[128,2,384]{2,1,0:T(2,128)(2,1)} %reshape.34), calls=%async_computation.1 | async-start | bytes 393216 | tf_op jit(solution)/shard_map/all_to_all | solution.py:424
  97.0 0.0 copy-done.6
  97.1 0.0 copy-start.9
  97.1 0.7 copy-done.9
  97.8 0.0 copy-start.7
  97.8 0.0 copy-start.8
  97.8 0.0 copy-done
  97.8 0.0 copy-done.1
  97.8 0.0 copy-done.2
  97.8 0.0 copy-done.4
  97.8 0.0 copy-done.5
  97.8 0.6 copy-done.7
  98.4 0.0 copy-done.8
  98.4 1.0 gates.1
  99.5 14.9 %all-to-all-done.1 = bf16[128,2,384]{2,1,0:T(2,128)(2,1)S(1)} async-done(((bf16[128,2,384]{2,1,0:T(2,128)(2,1)}), bf16[128,2,384]{2,1,0:T(2,128)(2,1)S(1)}, u32[]{:S(2)}, u32[]{:S(2)}) %all-to-all-start.1) | async-done | bytes 196640 | tf_op jit(solution)/shard_map/all_to_all | solution.py:424
  114.4 1.6 after.1
  116.1 4.4 %all-to-all-start.2 = ((bf16[16,24,128]{2,1,0:T(8,128)(2,1)}), bf16[16,24,128]{2,1,0:T(8,128)(2,1)S(1)}, u32[]{:S(2)}, u32[]{:S(2)}) async-start(bf16[16,24,128]{2,1,0:T(8,128)(2,1)} %get-tuple-element.25), calls=%async_computation.2 | async-start | bytes 196608 | tf_op jit(solution)/shard_map/all_to_all | solution.py:431
  120.5 0.4 items.1
  120.8 11.3 %all-to-all-done.2 = bf16[16,24,128]{2,1,0:T(8,128)(2,1)S(1)} async-done(((bf16[16,24,128]{2,1,0:T(8,128)(2,1)}), bf16[16,24,128]{2,1,0:T(8,128)(2,1)S(1)}, u32[]{:S(2)}, u32[]{:S(2)}) %all-to-all-start.2) | async-done | bytes 98336 | tf_op jit(solution)/shard_map/all_to_all | solution.py:431
  132.1 0.3 pack.1
  132.4 24.9 %all_to_all.26.whole_ref = bf16[16,144,128]{2,1,0:T(8,128)(2,1)S(1)} all-to-all(bf16[16,144,128]{2,1,0:T(8,128)(2,1)S(1)} %bitcast.13), channel_id=1, replica_groups=mesh['grp'=2,'row'=16,'col'=8,'sub'=2] {'col','sub'}, dimensions={0} | all-to-all | bytes 1179648 | tf_op jit(solution)/shard_map/all_to_all | solution.py:445
  157.3 0.4 table.1
  157.7 2.1 %all_gather.7.bias_ref = bf16[384,384]{1,0:T(8,128)(2,1)S(1)} all-gather(bf16[192,384]{1,0:T(8,128)(2,1)S(1)} %table.1), channel_id=1, replica_groups=mesh['grp'=2,'row'=16,'col'=8,'sub'=2] {'sub'}, dimensions={0}, use_global_device_ids=true | all-gather | bytes 442368 | tf_op jit(solution)/shard_map/all_gather | solution.py:447
  159.7 1.8 %attend.1 = bf16[16,40,128]{2,1,0:T(8,128)(2,1)S(1)} custom-call(bf16[16,144,128]{2,1,0:T(8,128)(2,1)S(1)} %all_to_all.26.whole_ref, bf16[384,384]{1,0:T(8,128)(2,1)S(1)} %all_gather.7.bias_ref, f32[1,384]{1,0:T(1,128)S(1)} %reshape.36.live_ref), custom_call_target="tpu_custom_call" | custom-call | flops 4194304 | bytes 1048576 | tf_op jit(solution)/shard_map/attend/pallas_call | solution.py:54
  161.5 0.0 copy-start.3
  161.6 12.5 %all_to_all.27.back_ref = bf16[16,40,128]{2,1,0:T(8,128)(2,1)S(1)} all-to-all(bf16[16,40,128]{2,1,0:T(8,128)(2,1)S(1)} %attend.1), channel_id=1, replica_groups=mesh['grp'=2,'row'=16,'col'=8,'sub'=2] {'col','sub'}, dimensions={0} | all-to-all | bytes 327680 | tf_op jit(solution)/shard_map/all_to_all | solution.py:451
  174.1 0.0 copy-done.3
  174.1 1.0 finish.1
  (5 shorter events, 0.1 us)
Async XLA Ops:
  86.9 10.1 %copy-start.6 = (s32[384]{0:T(512)S(1)}, s32[384]{0:T(512)}, u32[]{:S(2)}) copy-start(s32[384]{0:T(512)} %live_ref.1) | copy-start | bytes 4612
  86.9 10.8 %copy-start = (bf16[24,24,128]{2,1,0:T(8,128)(2,1)S(1)}, bf16[24,24,128]{2,1,0:T(8,128)(2,1)}, u32[]{:S(2)}) copy-start(bf16[24,24,128]{2,1,0:T(8,128)(2,1)} %param.11) | copy-start | bytes 442372
  86.9 10.8 %copy-start.1 = (bf16[128,256]{1,0:T(8,128)(2,1)S(1)}, bf16[128,256]{1,0:T(8,128)(2,1)}, u32[]{:S(2)}) copy-start(bf16[128,256]{1,0:T(8,128)(2,1)} %query_ref.3) | copy-start | bytes 196612
  87.0 10.8 %copy-start.2 = (bf16[128,256]{1,0:T(8,128)(2,1)S(1)}, bf16[128,256]{1,0:T(8,128)(2,1)}, u32[]{:S(2)}) copy-start(bf16[128,256]{1,0:T(8,128)(2,1)} %keyval_ref.1) | copy-start | bytes 196612
  87.0 10.8 %copy-start.4 = (bf16[128,128]{1,0:T(8,128)(2,1)S(1)}, bf16[128,128]{1,0:T(8,128)(2,1)}, u32[]{:S(2)}) copy-start(bf16[128,128]{1,0:T(8,128)(2,1)} %tri_gate_ref.1) | copy-start | bytes 98308
  87.0 10.8 %copy-start.5 = (bf16[128,128]{1,0:T(8,128)(2,1)S(1)}, bf16[128,128]{1,0:T(8,128)(2,1)}, u32[]{:S(2)}) copy-start(bf16[128,128]{1,0:T(8,128)(2,1)} %tri_out_ref.1) | copy-start | bytes 98308
  87.0 27.4 %all-to-all-start.1 = ((bf16[128,2,384]{2,1,0:T(2,128)(2,1)}), bf16[128,2,384]{2,1,0:T(2,128)(2,1)S(1)}, u32[]{:S(2)}, u32[]{:S(2)}) async-start(bf16[128,2,384]{2,1,0:T(2,128)(2,1)} %reshape.34), calls=%async_computation.1 | async-start | bytes 393216 | tf_op jit(solution)/shard_map/all_to_all | solution.py:424
  97.1 0.7 copy-start.9
  97.8 0.7 copy-start.7
  97.8 0.7 copy-start.8
  116.1 16.0 %all-to-all-start.2 = ((bf16[16,24,128]{2,1,0:T(8,128)(2,1)}), bf16[16,24,128]{2,1,0:T(8,128)(2,1)S(1)}, u32[]{:S(2)}, u32[]{:S(2)}) async-start(bf16[16,24,128]{2,1,0:T(8,128)(2,1)} %get-tuple-element.25), calls=%async_computation.2 | async-start | bytes 196608 | tf_op jit(solution)/shard_map/all_to_all | solution.py:431
  161.5 12.5 %copy-start.3 = (bf16[128,128]{1,0:T(8,128)(2,1)S(1)}, bf16[128,128]{1,0:T(8,128)(2,1)}, u32[]{:S(2)}) copy-start(bf16[128,128]{1,0:T(8,128)(2,1)} %att_out_ref.1) | copy-start | bytes 98308

commit v6 on v4

--- a/solution.py
+++ b/solution.py
@@ -89,11 +89,12 @@
         copies = [pltpu.make_async_copy(a, b, c) for a, b, c in zip(outside, inside, sems)]
         for copy in copies:
             copy.start()
-        for copy in copies:
+        for copy in copies[:4]:
             copy.wait()
         pair_ref, chain_ref, live_ref, vec_ref, tri_in_ref = inside
         start, mask = start_block(pair_ref, chain_ref, live_ref, place_ref, vec_ref, rows, cols)
         normed = normalised(start).astype(BF16).astype(F32) * mask
+        copies[4].wait()
         weights = tri_in_ref[...].astype(F32).T.astype(BF16)
         width = send_ref.shape[0]
         for t in range(tiles):
@@ -422,13 +423,14 @@
         (returned.reshape(channels, rows // 4 * LANES), start, tri_gating, near_out, wide_bias),
         "vvvvv",
     )
-    columns = lax.all_to_all(copies, "row", split_axis=0, concat_axis=0, tiled=True)
     plain_items, gating = call(
         items_kernel(positions),
         [((HEADS * positions, LANES), BF16), ((positions, channels), F32)],
         (second, head_weights, att_query),
         "vvv",
     )
+    copies, plain_items, gating = lax.optimization_barrier((copies, plain_items, gating))
+    columns = lax.all_to_all(copies, "row", split_axis=0, concat_axis=0, tiled=True)
     chunk = items * cols
     (sent_items,) = call(
         pack_kernel(chunk, cols, length, nsub),

time: 175 us -> 174 us (level)
  blocking collectives: 121 us -> 137 us
  waiting for transfers between devices: 25.7 us -> 14.4 us
  starting transfers between devices: 14.8 us -> 10 us
    all_to_all x0 -> x1, blocking collectives: none -> 16.3 us  [on_device(): lax.all_to_all(copies, 'row', split_axis=0, concat_axis=0, tiled=True)]
    all_to_all x1 -> x0, waiting for transfers between devices: 11.3 us -> none  [on_device(): lax.all_to_all(copies, 'row', split_axis=0, concat_axis=0, tiled=True)]
    all_to_all x1 -> x0, starting transfers between devices: 4.78 us -> none  [on_device(): lax.all_to_all(copies, 'row', split_axis=0, concat_axis=0, tiled=True)]
  transfers between devices with their start and end apart: 2 -> 1, of which waited for: 2 -> 1; matrix products, arithmetic and copies ran while one was open for 0% -> 0% of each run, Pallas kernels for 1% -> 1%
where the time goes in v6:
time: 174 us
  blocking collectives  137 us (79%)
  waiting for transfers between devices  14.4 us (8%)
  starting transfers between devices  10 us (6%)
  Pallas kernels  9.79 us (6%)
  local copies, waits for them, and re-layouts  2.22 us (1%)
    all_to_all x1, blocking collectives, on_device(): lax.all_to_all(send.reshape(channels, 2, tiles * LANES), ('col', 'row'),...  76.1 us
    all_to_all x1, blocking collectives, on_device(): lax.all_to_all(sent_items.reshape(blocks, chunk, LANES), ('col', 'sub'),...  24.6 us
    all_to_all x1, blocking collectives, on_device(): lax.all_to_all(copies, 'row', split_axis=0, concat_axis=0, tiled=True)  16.3 us
    all_to_all x1, waiting for transfers between devices, on_device(): lax.all_to_all(products.reshape(nrow * ncol, 2, rows // 8 * LANES), ('col...  14.4 us
    all_to_all x1, blocking collectives, on_device(): lax.all_to_all(attended, ('col', 'sub'), split_axis=0, concat_axis=0, til...  12.5 us
    all_to_all x1, starting transfers between devices, on_device(): lax.all_to_all(products.reshape(nrow * ncol, 2, rows // 8 * LANES), ('col...  10 us
    pallas_call x9, Pallas kernels, call(): pl.pallas_call(kernel, out_shape=[jax.ShapeDtypeStruct(s, t) for s, t in...  9.79 us
    all_gather x1, blocking collectives, on_device(): lax.all_gather(moved.reshape(channels, 2 * tiles * LANES), 'sub', axis=0,...  5.64 us
  transfers between devices with their start and end apart: 1, of which 1 were waited for; matrix products, arithmetic and copies ran while one was open for 0% of the time, Pallas kernels for 1%

profile of v6, /device:TPU:65, one launch (start us, length us, event | category | flops | bytes accessed | tf_op | source)
XLA Modules:
  0.0 173.9 jit_solution(5099253823861545043)
XLA Ops:
  0.0 0.1 pad_add_fusion.place_ref
  0.1 2.2 %sides.1 = bf16[128,1280]{1,0:T(8,128)(2,1)S(1)} custom-call(s32[3]{0:T(128)S(1)} %pad_add_fusion.place_ref, bf16[576,128]{1,0:T(8,128)(2,1)} %bitcast.15, s32[384]{0:T(512)} %chain_ref.1, s32[384]{0:T(512)} %live_ref.1, f32[1,128]{1,0:T(1,128)} %bitcast.18, bf16[128,512]{1,0:T(8,128)(2,1)} %refs_4_.1), custom_call_target="tpu_custom_call" | custom-call | flops 4194304 | bytes 1048576 | tf_op jit(solution)/shard_map/sides/pallas_call | solution.py:54
  2.3 0.1 reshape.32
  2.4 76.1 %all_to_all.25 = bf16[128,2,640]{2,1,0:T(2,128)(2,1)S(1)} all-to-all(bf16[128,2,640]{2,1,0:T(2,128)(2,1)S(1)} %reshape.32), channel_id=1, replica_groups=mesh['grp'=2,'row'=16,'col'=8,'sub'=2] {'col','row'}, dimensions={0} | all-to-all | bytes 655360 | tf_op jit(solution)/shard_map/all_to_all | solution.py:393
  78.6 5.6 %all_gather.6.gathered_ref = bf16[256,1280]{1,0:T(8,128)(2,1)S(1)} all-gather(bf16[128,1280]{1,0:T(8,128)(2,1)S(1)} %bitcast.21), channel_id=1, replica_groups=mesh['grp'=2,'row'=16,'col'=8,'sub'=2] {'sub'}, dimensions={0}, use_global_device_ids=true | all-gather | bytes 983040 | tf_op jit(solution)/shard_map/all_gather | solution.py:408
  84.2 1.8 %products.1 = bf16[128,768]{1,0:T(8,128)(2,1)S(1)} custom-call(s32[3]{0:T(128)S(1)} %pad_add_fusion.place_ref, bf16[256,1280]{1,0:T(8,128)(2,1)S(1)} %all_gather.6.gathered_ref), custom_call_target="tpu_custom_call" | custom-call | flops 4194304 | bytes 1048576 | tf_op jit(solution)/shard_map/products/pallas_call | solution.py:54
  86.0 0.7 reshape.34
  86.7 0.0 copy-start.6
  86.7 0.0 copy-start
  86.7 0.0 copy-start.1
  86.7 0.0 copy-start.2
  86.7 0.0 copy-start.4
  86.7 0.0 copy-start.5
  86.8 10.0 %all-to-all-start.1 = ((bf16[128,2,384]{2,1,0:T(2,128)(2,1)}), bf16[128,2,384]{2,1,0:T(2,128)(2,1)S(1)}, u32[]{:S(2)}, u32[]{:S(2)}) async-start(bf16[128,2,384]{2,1,0:T(2,128)(2,1)} %reshape.34), calls=%async_computation.1 | async-start | bytes 393216 | tf_op jit(solution)/shard_map/all_to_all | solution.py:419
  96.8 0.0 copy-done.6
  96.8 0.0 copy-start.9
  96.8 0.7 copy-done.9
  97.5 0.0 copy-start.7
  97.5 0.0 copy-start.8
  97.5 0.0 copy-done
  97.5 0.0 copy-done.1
  97.5 0.0 copy-done.2
  97.5 0.0 copy-done.4
  97.5 0.0 copy-done.5
  97.6 0.6 copy-done.7
  98.2 0.0 copy-done.8
  98.2 1.0 gates.1
  99.2 14.4 %all-to-all-done.1 = bf16[128,2,384]{2,1,0:T(2,128)(2,1)S(1)} async-done(((bf16[128,2,384]{2,1,0:T(2,128)(2,1)}), bf16[128,2,384]{2,1,0:T(2,128)(2,1)S(1)}, u32[]{:S(2)}, u32[]{:S(2)}) %all-to-all-start.1) | async-done | bytes 196640 | tf_op jit(solution)/shard_map/all_to_all | solution.py:419
  113.6 1.0 after.1
  114.6 0.4 items.1
  115.0 16.3 %all_to_all.26 = bf16[16,24,128]{2,1,0:T(8,128)(2,1)S(1)} all-to-all(bf16[16,24,128]{2,1,0:T(8,128)(2,1)S(1)} %get-tuple-element.31), channel_id=1, replica_groups=mesh['grp'=2,'row'=16,'col'=8,'sub'=2] {'row'}, dimensions={0} | all-to-all | bytes 196608 | tf_op jit(solution)/shard_map/all_to_all | solution.py:433
  131.2 0.3 pack.1
  131.5 24.6 %all_to_all.27.whole_ref = bf16[16,144,128]{2,1,0:T(8,128)(2,1)S(1)} all-to-all(bf16[16,144,128]{2,1,0:T(8,128)(2,1)S(1)} %bitcast.13), channel_id=1, replica_groups=mesh['grp'=2,'row'=16,'col'=8,'sub'=2] {'col','sub'}, dimensions={0} | all-to-all | bytes 1179648 | tf_op jit(solution)/shard_map/all_to_all | solution.py:441
  156.1 0.4 table.1
  156.5 2.1 %all_gather.7.bias_ref = bf16[384,384]{1,0:T(8,128)(2,1)S(1)} all-gather(bf16[192,384]{1,0:T(8,128)(2,1)S(1)} %table.1), channel_id=1, replica_groups=mesh['grp'=2,'row'=16,'col'=8,'sub'=2] {'sub'}, dimensions={0}, use_global_device_ids=true | all-gather | bytes 442368 | tf_op jit(solution)/shard_map/all_gather | solution.py:443
  158.6 1.8 %attend.1 = bf16[16,40,128]{2,1,0:T(8,128)(2,1)S(1)} custom-call(bf16[16,144,128]{2,1,0:T(8,128)(2,1)S(1)} %all_to_all.27.whole_ref, bf16[384,384]{1,0:T(8,128)(2,1)S(1)} %all_gather.7.bias_ref, f32[1,384]{1,0:T(1,128)S(1)} %reshape.36.live_ref), custom_call_target="tpu_custom_call" | custom-call | flops 4194304 | bytes 1048576 | tf_op jit(solution)/shard_map/attend/pallas_call | solution.py:54
  160.4 0.0 copy-start.3
  160.4 12.5 %all_to_all.28.back_ref = bf16[16,40,128]{2,1,0:T(8,128)(2,1)S(1)} all-to-all(bf16[16,40,128]{2,1,0:T(8,128)(2,1)S(1)} %attend.1), channel_id=1, replica_groups=mesh['grp'=2,'row'=16,'col'=8,'sub'=2] {'col','sub'}, dimensions={0} | all-to-all | bytes 327680 | tf_op jit(solution)/shard_map/all_to_all | solution.py:447
  172.9 0.0 copy-done.3
  172.9 1.0 finish.1
  (5 shorter events, 0.1 us)
Async XLA Ops:
  86.7 10.1 %copy-start.6 = (s32[384]{0:T(512)S(1)}, s32[384]{0:T(512)}, u32[]{:S(2)}) copy-start(s32[384]{0:T(512)} %live_ref.1) | copy-start | bytes 4612
  86.7 10.8 %copy-start = (bf16[24,24,128]{2,1,0:T(8,128)(2,1)S(1)}, bf16[24,24,128]{2,1,0:T(8,128)(2,1)}, u32[]{:S(2)}) copy-start(bf16[24,24,128]{2,1,0:T(8,128)(2,1)} %param.11) | copy-start | bytes 442372
  86.7 10.8 %copy-start.1 = (bf16[128,256]{1,0:T(8,128)(2,1)S(1)}, bf16[128,256]{1,0:T(8,128)(2,1)}, u32[]{:S(2)}) copy-start(bf16[128,256]{1,0:T(8,128)(2,1)} %query_ref.3) | copy-start | bytes 196612
  86.7 10.8 %copy-start.2 = (bf16[128,256]{1,0:T(8,128)(2,1)S(1)}, bf16[128,256]{1,0:T(8,128)(2,1)}, u32[]{:S(2)}) copy-start(bf16[128,256]{1,0:T(8,128)(2,1)} %keyval_ref.1) | copy-start | bytes 196612
  86.7 10.8 %copy-start.4 = (bf16[128,128]{1,0:T(8,128)(2,1)S(1)}, bf16[128,128]{1,0:T(8,128)(2,1)}, u32[]{:S(2)}) copy-start(bf16[128,128]{1,0:T(8,128)(2,1)} %tri_gate_ref.1) | copy-start | bytes 98308
  86.7 10.8 %copy-start.5 = (bf16[128,128]{1,0:T(8,128)(2,1)S(1)}, bf16[128,128]{1,0:T(8,128)(2,1)}, u32[]{:S(2)}) copy-start(bf16[128,128]{1,0:T(8,128)(2,1)} %tri_out_ref.1) | copy-start | bytes 98308
  86.8 26.8 %all-to-all-start.1 = ((bf16[128,2,384]{2,1,0:T(2,128)(2,1)}), bf16[128,2,384]{2,1,0:T(2,128)(2,1)S(1)}, u32[]{:S(2)}, u32[]{:S(2)}) async-start(bf16[128,2,384]{2,1,0:T(2,128)(2,1)} %reshape.34), calls=%async_computation.1 | async-start | bytes 393216 | tf_op jit(solution)/shard_map/all_to_all | solution.py:419
  96.8 0.7 copy-start.9
  97.5 0.7 copy-start.7
  97.5 0.7 copy-start.8
  160.4 12.5 %copy-start.3 = (bf16[128,128]{1,0:T(8,128)(2,1)S(1)}, bf16[128,128]{1,0:T(8,128)(2,1)}, u32[]{:S(2)}) copy-start(bf16[128,128]{1,0:T(8,128)(2,1)} %att_out_ref.1) | copy-start | bytes 98308
